TPU v7x, 256 devices: a whole 4x4x8 slice. The times are simulated.
256 devices in a mesh: dp: 32 (over y, z), mp: 8 (over x, core).
Axes of the slice: x: 4, y: 4, z: 8, core: 2. Of those that a mesh axis runs over, the one named last changes fastest.
Arguments:
- tokens: bfloat16 [32, 1024, 1280], P('dp', 'mp'), may hold values from -6 to 6
- sizes: float32 [32, 1024], P('dp'), may hold values from 1 to 8
- ln1_gain: float32 [1280], replicated, may hold values from 0.25 to 1.75
- qkv_weight: bfloat16 [3, 1280, 1280], P(None, 'dp', 'mp'), may hold values from -0.15625 to 0.15625
- proj_weight: bfloat16 [1280, 1280], P('mp', 'dp'), may hold values from -0.15625 to 0.15625
- ln2_gain: float32 [1280], replicated, may hold values from 0.25 to 1.75
- fc1_weight: bfloat16 [1280, 5120], P('dp', 'mp'), may hold values from -0.15625 to 0.15625
- fc1_bias: float32 [5120], P('mp'), may hold values from -3 to 3
- fc2_weight: bfloat16 [5120, 1280], P('mp', 'dp'), may hold values from -0.078125 to 0.078125
- pair_source: int32 [32, 16], P('dp'), may hold values from 0 to 1022, as said below
- pair_target: int32 [32, 16], P('dp'), may hold values from 1 to 1023, as said below
- kept_order: int32 [32, 1008], P('dp'), may hold values from 0 to 1023, as said below
Outputs:
- merged_out: bfloat16 [32, 1008, 1280], P('dp', 'mp')
Inputs may be any that keep to these rules, and one draw needn't show every extreme that they name: `pair_source`: in each image the 16 entries are distinct even token indices. `pair_target`: odd token indices; several sources may join the same target. `kept_order`: in each image every token index that is not in pair_source appears exactly once.
All inputs are finite; a program needn't handle non-finite values.
Results may differ from a plain program's by a relative error of at most 0.017.
Values may be sent and summed in bfloat16 or wider, within the bound.
No kernel may reach another device: no remote copies, remote signals or barrier semaphores. Data moves between devices by JAX's collectives and lax.ppermute only.
A program may use at most 64 MiB of HBM per device.

v0:
```python
import functools
import math

import jax
import jax.numpy as jnp
from jax import lax
from jax.experimental import pallas as pl
from jax.experimental.pallas import tpu as pltpu
from jax.sharding import Mesh, PartitionSpec as P

HEADS = 16
BF = jnp.bfloat16
F32 = jnp.float32
VMEM = pltpu.VMEM
SMEM = pltpu.SMEM


def shift(x, axis, by):
    n = lax.axis_size(axis)
    return lax.ppermute(x, axis, [(i, (i + by) % n) for i in range(n)])


def layer_norm(values, gain):
    center = values - jnp.mean(values, axis=-1, keepdims=True)
    spread = jnp.mean(center * center, axis=-1, keepdims=True)
    return center * lax.rsqrt(spread + 1e-06) * gain


def dot_t(a, b):
    return lax.dot_general(a, b, (((1,), (1,)), ((), ())), preferred_element_type=F32)


def dot(a, b):
    return jnp.dot(a, b, preferred_element_type=F32)


def whole(n, space=VMEM):
    return [pl.BlockSpec(memory_space=space)] * n


def params(mib):
    return pltpu.CompilerParams(vmem_limit_bytes=mib * 2**20)


def cost(flops, nbytes):
    return pl.CostEstimate(flops=int(flops), bytes_accessed=int(nbytes), transcendentals=0)


def norm_kernel(gain_ref, *refs):
    blocks, (raw_ref, out_ref) = refs[:-2], refs[-2:]
    step = 64
    for n, block in enumerate(blocks):
        rows = block.shape[0]

        @pl.loop(0, rows // step)
        def _(i):
            at = pl.multiple_of(i * step, step)
            x = block[pl.ds(at, step), :]
            raw_ref[pl.ds(n * rows + at, step), :] = x
            out_ref[pl.ds(n * rows + at, step), :] = layer_norm(x.astype(F32), gain_ref[...]).astype(BF)


def norm_other_kernel(gain_ref, block, out_ref):
    step = 64

    @pl.loop(0, block.shape[0] // step)
    def _(i):
        at = pl.ds(pl.multiple_of(i * step, step), step)
        out_ref[at, :] = layer_norm(block[at, :].astype(F32), gain_ref[...]).astype(BF)


def norms(gain, blocks):
    rows = sum(b.shape[0] for b in blocks)
    shape = jax.ShapeDtypeStruct((rows, blocks[0].shape[1]), BF)
    return pl.pallas_call(
        norm_kernel,
        out_shape=[shape, shape],
        in_specs=whole(1 + len(blocks)),
        out_specs=whole(2),
        compiler_params=params(16),
        cost_estimate=cost(2e9, 4e6),
        name="norm_mine",
    )(gain, *blocks)


def norm_other(gain, block):
    return pl.pallas_call(
        norm_other_kernel,
        out_shape=jax.ShapeDtypeStruct(block.shape, BF),
        in_specs=whole(2),
        out_specs=whole(1)[0],
        compiler_params=params(16),
        cost_estimate=cost(2e9, 3e6),
        name="norm_other",
    )(gain, block)


def place(blocks, scratch, sems, first, left=0):
    rows = blocks[0].shape[0]
    right = left + scratch.shape[1]
    copies = []
    for j, block in enumerate(blocks):
        start = pl.multiple_of(lax.rem(first + j, len(blocks)) * rows, 64)
        copies.append(pltpu.make_async_copy(block.at[:, left:right], scratch.at[pl.ds(start, rows), :], sems.at[j]))
    for copy in copies:
        copy.start()
    return copies


def attention_kernel(hs, y_ref, xa_ref, xb_ref, w0, w1, w2, w3, kx_ref, keep_ref, send_ref,
                     out_keep, out_send, w_scr, qkv_scr, q_scr, k_scr, v_scr, att_scr, sems):
    half = xa_ref.shape[0]
    tokens = 2 * half
    for copy in place((w0, w1, w2, w3), w_scr, sems, y_ref[0]):
        copy.wait()
    chunk = 256
    qkv_scr[:half, :] = dot(xa_ref[...], w_scr[...])
    qkv_scr[half:, :] = dot(xb_ref[...], w_scr[...])
    scale = math.log2(math.e) / math.sqrt(hs)

    def piece(j):
        first, offset = divmod(hs * j, 128)
        width = 128 if offset + hs <= 128 else 256
        x = qkv_scr[:, 128 * first : 128 * first + width]
        if offset:
            x = pltpu.roll(x, width - offset, 1)
        return x[:, :128]

    lane = lax.broadcasted_iota(jnp.int32, (tokens, 128), 1)
    real = lane < hs
    for h in range(2):
        ones = jnp.where(lane < hs + 3, 1.0, 0.0)
        q_scr[h] = jnp.where(real, piece(h), ones).astype(BF)
        k_scr[h] = jnp.where(real, piece(2 + h), kx_ref[...]).astype(BF)
        v_scr[h] = jnp.where(real, piece(4 + h), ones).astype(BF)

    @pl.loop(0, 2)
    def _(h):
        for r in range(0, tokens, chunk):
            s = dot_t(q_scr[h, r : r + chunk, :], k_scr[h])
            top = jnp.max(s, axis=-1, keepdims=True)
            p = jnp.exp2((s - top) * scale).astype(BF)
            o = dot(p, v_scr[h])
            o = o / o[:, hs : hs + 1]
            o = jnp.where(lane[:chunk] < hs, o, 0.0)
            att_scr[r : r + chunk, pl.ds(pl.multiple_of(128 * h, 128), 128)] = o.astype(BF)

    out_send[...] = dot(send_ref[...], att_scr[...]).astype(BF)
    out_keep[...] = dot(keep_ref[...], att_scr[...]).astype(BF)


def attention(y, xa, xb, blocks, kx, keep, send, hs):
    tokens = 2 * xa.shape[0]
    rows = keep.shape[0]
    return pl.pallas_call(
        functools.partial(attention_kernel, hs),
        out_shape=[jax.ShapeDtypeStruct((rows, 256), BF)] * 2,
        in_specs=whole(1, SMEM) + whole(2) + whole(4, pl.ANY) + whole(3),
        out_specs=whole(2),
        scratch_shapes=[
            pltpu.VMEM((4 * blocks[0].shape[0], 512), BF),
            pltpu.VMEM((tokens, 512), F32),
            pltpu.VMEM((2, tokens, 128), BF),
            pltpu.VMEM((2, tokens, 128), BF),
            pltpu.VMEM((2, tokens, 128), BF),
            pltpu.VMEM((tokens, 256), BF),
            pltpu.SemaphoreType.DMA((4,)),
        ],
        compiler_params=params(40),
        cost_estimate=cost(8e9, 8e6),
        name="attention",
    )(y, xa, xb, *blocks, kx, keep, send)


def proj_weight_kernel(hs, y_ref, w0, w1, w2, w3, out_ref, w_scr, sems):
    for copy in place((w0, w1, w2, w3), w_scr, sems, y_ref[0], 384):
        copy.wait()
    step = 320
    lane = lax.broadcasted_iota(jnp.int32, (step, 128), 1)

    @pl.loop(0, w_scr.shape[0] // step)
    def _(i):
        at = pl.ds(pl.multiple_of(i * step, step), step)
        x = w_scr[at, :].astype(F32)
        for h in range(2):
            turn = 256 - (96 + hs * h)
            p = jnp.where(lane < hs, pltpu.roll(x, turn, 1)[:, :128], 0.0)
            out_ref[at, 128 * h : 128 * h + 128] = p.astype(BF)


def proj_weights(y, blocks, hs):
    rows = blocks[0].shape[0]
    return pl.pallas_call(
        functools.partial(proj_weight_kernel, hs),
        out_shape=jax.ShapeDtypeStruct((4 * rows, 256), BF),
        in_specs=whole(1, SMEM) + whole(4, pl.ANY),
        out_specs=whole(1)[0],
        scratch_shapes=[pltpu.VMEM((4 * rows, 256), BF), pltpu.SemaphoreType.DMA((4,))],
        compiler_params=params(16),
        cost_estimate=cost(1e9, 3e6),
        name="proj_weights",
    )(y, *blocks)


def projection_kernel(kept, other, w_kept, w_other, base, mine, *sent):
    part = dot_t(kept[...], w_kept[...]) + dot_t(other[...], w_other[...])
    mine[...] = base[...] + part[:128]
    for k, out in enumerate(sent):
        out[...] = part[128 * (k + 1) : 128 * (k + 2)].astype(BF)


def projection(kept, other, w_kept, w_other, base):
    return pl.pallas_call(
        projection_kernel,
        out_shape=[jax.ShapeDtypeStruct(base.shape, F32)] + [jax.ShapeDtypeStruct(base.shape, BF)] * 3,
        in_specs=whole(5),
        out_specs=whole(4),
        compiler_params=params(16),
        cost_estimate=cost(1e9, 4e6),
        name="projection",
    )(kept, other, w_kept, w_other, base)


def merged_kernel(gain, mine, a, b, d, merged_ref, out_ref):
    merged = mine[...] + a[...].astype(F32) + b[...].astype(F32) + d[...].astype(F32)
    merged_ref[...] = merged
    out_ref[...] = layer_norm(merged, gain[...]).astype(BF)


def merged_norm(gain, mine, received):
    return pl.pallas_call(
        merged_kernel,
        out_shape=[jax.ShapeDtypeStruct(mine.shape, F32), jax.ShapeDtypeStruct(mine.shape, BF)],
        in_specs=whole(5),
        out_specs=whole(2),
        compiler_params=params(16),
        cost_estimate=cost(1e8, 2e6),
        name="merged_norm",
    )(gain, mine, *received)


def mlp_weights_kernel(yz_ref, *refs):
    *blocks, up, down = refs
    half = up.shape[2]
    zs = len(blocks)
    y, z = yz_ref[0], yz_ref[1]
    ys = blocks[0].shape[0]
    for k, block in enumerate(blocks):
        for j in range(ys):
            at = lax.rem(y + j, ys) * zs + lax.rem(z + k, zs)
            up[at] = block[j, :, :half]
            down[at] = block[j, :, half:]


def mlp_weights(yz, blocks):
    ys, rows, cols = blocks[0].shape
    total = ys * len(blocks)
    return pl.pallas_call(
        mlp_weights_kernel,
        out_shape=[jax.ShapeDtypeStruct((total, rows, cols // 2), BF)] * 2,
        in_specs=whole(1, SMEM) + whole(len(blocks)),
        out_specs=whole(2),
        compiler_params=params(16),
        cost_estimate=cost(1e9, 6e6),
        name="mlp_weights",
    )(yz, *blocks)


def mlp_kernel(n, *refs):
    ins, (up_a, up_b, down_a, down_b, bias_a, bias_b) = refs[:n], refs[n : n + 6]
    outs, (rows, hidden) = refs[n + 6 : 2 * n + 6], refs[2 * n + 6 :]
    for k, r in enumerate(ins):
        rows[128 * k : 128 * k + 128, :] = r[...]
    half = up_a.shape[1]
    for i, (up, bias) in enumerate(((up_a, bias_a), (up_b, bias_b))):
        h = jax.nn.gelu(dot(rows[...], up[...]) + bias[...])
        hidden[:, half * i : half * (i + 1)] = h.astype(BF)
    total = dot_t(hidden[:, :half], down_a[...]) + dot_t(hidden[:, half:], down_b[...])
    for k, out in enumerate(outs):
        out[...] = total[128 * k : 128 * k + 128].astype(out.dtype)


def mlp(rows, ups, downs, biases, kind):
    shape = rows[0].shape
    n = len(rows)
    return pl.pallas_call(
        functools.partial(mlp_kernel, n),
        out_shape=[jax.ShapeDtypeStruct(shape, kind)] * n,
        in_specs=whole(n + 6),
        out_specs=whole(n),
        scratch_shapes=[
            pltpu.VMEM((n * shape[0], shape[1]), BF),
            pltpu.VMEM((n * shape[0], 2 * ups[0].shape[1]), BF),
        ],
        compiler_params=params(24),
        cost_estimate=cost(1.5e9 * n, 8e6),
    )(*rows, *ups, *downs, *(b[None] for b in biases))


def turned(table, x, c):
    blocks = table.reshape(4, 2, 128)
    blocks = lax.dynamic_slice_in_dim(jnp.concatenate([blocks, blocks]), x, 4, 0)
    mine = lax.dynamic_index_in_dim(blocks, c, 1, keepdims=False)
    other = lax.dynamic_index_in_dim(blocks, 1 - c, 1, keepdims=False)
    return jnp.concatenate([mine.reshape(-1), other.reshape(-1)])


def tables(sizes, sources, targets, order, x, c, hs):
    kept = order.shape[0] // 8
    positions = jnp.arange(1024, dtype=jnp.int32)
    hits = positions[None, :] == sources[:, None]
    dest = positions + jnp.sum(jnp.where(hits, targets[:, None] - positions[None, :], 0), axis=0)
    dest = turned(dest, x, c)
    size = turned(sizes, x, c)
    order = jnp.pad(order.reshape(8, kept), ((0, 0), (0, 128 - kept)), constant_values=-1)
    order = turned(order.reshape(-1), x, c).reshape(2, 512)
    table = jnp.where(order[:, :, None] == dest, size, 0.0)
    merged_size = jnp.sum(table, axis=-1, keepdims=True)
    table = (table / jnp.where(merged_size == 0.0, 1.0, merged_size)).astype(BF)
    bias = jnp.log(size) * math.sqrt(hs)
    high = lax.reduce_precision(bias, 8, 7)
    mid = lax.reduce_precision(bias - high, 8, 7)
    low = bias - high - mid
    lane = jnp.arange(128)[None, :] - hs
    kx = jnp.where(lane == 0, high[:, None], jnp.where(lane == 1, mid[:, None], jnp.where(lane == 2, low[:, None], 0.0)))
    return table[0], table[1], kx


def shards(tokens, sizes, ln1_gain, qkv_weight, proj_weight, ln2_gain, fc1_weight,
           fc1_bias, fc2_weight, pair_source, pair_target, kept_order):
    y, z, x, c = (lax.axis_index(a) for a in ("y", "z", "x", "c"))
    zs = lax.axis_size("z")
    width = tokens.shape[2]
    hs = width // HEADS
    own = tokens[0]
    kept = kept_order.shape[1] // 8
    at_y = y[None]

    near = [own] + [shift(own, "x", -k) for k in (1, 2, 3)]
    raw_mine, normed_mine = norms(ln1_gain[None], near)
    raw_other = shift(raw_mine, "c", 1)
    normed_other = norm_other(ln1_gain[None], raw_other)

    qkvp = jnp.concatenate([qkv_weight[0], qkv_weight[1], qkv_weight[2], proj_weight.T], axis=1)
    by_z = lax.all_to_all(jnp.broadcast_to(qkvp, (zs, *qkvp.shape)), "z", 0, 0, tiled=True)
    by_z = by_z.reshape(-1, qkvp.shape[1])
    by_y = [by_z] + [shift(by_z, "y", -j) for j in (1, 2, 3)]

    updown = jnp.concatenate([fc1_weight, fc2_weight.T], axis=1)
    stack = jnp.stack([updown] + [shift(updown, "y", -j) for j in (1, 2, 3)])
    ring = {0: stack}
    for k in range(1, 4):
        ring[k] = shift(ring[k - 1], "z", -1)
        ring[zs - k] = shift(ring[(zs - k + 1) % zs], "z", 1)
    ring[zs // 2] = shift(ring[zs // 2 - 1], "z", -1)
    up, down = mlp_weights(jnp.stack([y, z]), [ring[k] for k in range(zs)])
    up = up.reshape(width, -1)
    down = down.reshape(width, -1)
    ups = (up, shift(up, "c", 1))
    downs = (down, shift(down, "c", 1))
    biases = (fc1_bias, shift(fc1_bias, "c", 1))

    keep, send, kx = tables(sizes[0], pair_source[0], pair_target[0], kept_order[0], x, c, hs)
    base = dot(keep[:128, :512], raw_mine) + dot(keep[:128, 512:], raw_other)

    proj = proj_weights(at_y, by_y, hs)
    proj_other = shift(proj, "c", 1)
    kept_rows, sent_rows = attention(at_y, normed_mine, normed_other, by_y, kx, keep, send, hs)
    other_rows = shift(sent_rows, "c", 1)

    mine, *sent = projection(kept_rows, other_rows, proj, proj_other, base)
    received = [shift(sent[k], "x", k + 1) for k in range(3)]
    merged, normed2 = merged_norm(ln2_gain[None], mine, received)
    rows = [shift(normed2, "x", -k) for k in (1, 2, 3)]
    (mine,) = mlp([normed2], ups, downs, biases, F32)
    first, third = mlp([rows[0], rows[2]], ups, downs, biases, BF)
    (second,) = mlp([rows[1]], ups, downs, biases, BF)
    received = [shift(b, "x", k).astype(F32) for k, b in ((1, first), (3, third), (2, second))]
    out = merged + mine + received[0] + received[1] + received[2]
    return out[:kept].astype(BF)[None]


def solution(mesh):
    fine = Mesh(mesh.devices.reshape(4, 8, 4, 2), ("y", "z", "x", "c"))
    dp, mp = ("y", "z"), ("x", "c")
    return jax.shard_map(
        shards,
        mesh=fine,
        in_specs=(
            P(dp, mp, None),
            P(dp, None),
            P(),
            P(None, dp, mp),
            P(mp, dp),
            P(),
            P(dp, mp),
            P(mp),
            P(mp, dp),
            P(dp, None),
            P(dp, None),
            P(dp, None),
        ),
        out_specs=P(dp, mp, None),
        check_vma=False,
    )
```

profile of v0, /device:TPU:1, one launch (start us, length us, event | category | flops | bytes accessed | tf_op | source)
XLA Modules:
  0.0 145.6 jit_solution(13230359351534770021)
XLA Ops:
  0.0 3.3 %collective-permute-start = (bf16[128,1280]{1,0:T(8,128)(2,1)}, bf16[128,1280]{1,0:T(8,128)(2,1)S(1)}, u32[]{:S(2)}, u32[]{:S(2)}) collective-permute-start(bf16[128,1280]{1,0:T(8,128)(2,1)} %bitcast.48), channel_id=1, source_target_pairs={{0,6},{2,0},{4,2},{6,4},{1,7},{3,1},{5,3},{7,5},{8,14},{10,8},{12,... | collective-permute-start | bytes 983048 | tf_op jit(solution)/shard_map/ppermute | solution.py:20
  4.7 2.8 %collective-permute-start.12 = (bf16[40,1280]{1,0:T(8,128)(2,1)S(1)}, bf16[40,1280]{1,0:T(8,128)(2,1)S(1)}, u32[]{:S(2)}, u32[]{:S(2)}) collective-permute-start(bf16[40,1280]{1,0:T(8,128)(2,1)S(1)} %get-tuple-element.36), channel_id=1, source_target_pairs={{0,192},{64,0},{128,64},{192,128},{1,193},{65,1},{129,65},{193,129... | collective-permute-start | bytes 307208 | tf_op jit(solution)/shard_map/ppermute | solution.py:20
  10.9 8.2 %all-to-all-start = ((bf16[8,40,640]{2,1,0:T(8,128)(2,1)}), bf16[8,40,640]{2,1,0:T(8,128)(2,1)}, u32[]{:S(2)}, u32[]{:S(2)}) async-start(bf16[8,40,640]{2,1,0:T(8,128)(2,1)} %broadcast_in_dim.99), calls=%async_computation | async-start | bytes 819200 | tf_op jit(solution)/shard_map/all_to_all | solution.py:345
  24.7 2.8 %collective-permute-start.15 = (bf16[4,40,1280]{2,1,0:T(8,128)(2,1)S(1)}, bf16[4,40,1280]{2,1,0:T(8,128)(2,1)S(1)}, u32[]{:S(2)}, u32[]{:S(2)}) collective-permute-start(bf16[4,40,1280]{2,1,0:T(8,128)(2,1)S(1)} %pad_maximum_fusion.refs_0_), channel_id=1, source_target_pairs={{0,56},{8,0},{16,8},{24,16},{32,24},{40,32},{48,40},{56,48},{1,57}... | collective-permute-start | bytes 1228808 | tf_op jit(solution)/shard_map/ppermute | solution.py:20
  27.5 4.9 %collective-permute-done.2.refs_3_ = bf16[128,1280]{1,0:T(8,128)(2,1)S(1)} collective-permute-done((bf16[128,1280]{1,0:T(8,128)(2,1)}, bf16[128,1280]{1,0:T(8,128)(2,1)S(1)}, u32[]{:S(2)}, u32[]{:S(2)}) %collective-permute-start.2) | collective-permute-done | bytes 327712 | tf_op jit(solution)/shard_map/ppermute | solution.py:20
  32.4 1.8 %norm_mine.1 = (bf16[512,1280]{1,0:T(8,128)(2,1)S(1)}, bf16[512,1280]{1,0:T(8,128)(2,1)S(1)}) custom-call(f32[1,1280]{1,0:T(1,128)S(1)} %broadcast_in_dim.98.gain_ref, bf16[128,1280]{1,0:T(8,128)(2,1)S(1)} %bitcast.51, bf16[128,1280]{1,0:T(8,128)(2,1)S(1)} %collective-permute-done.refs_1_, bf16[128,1280]{1,0:T(8,128)(2,1)S(1)} %collective-permute-done.1.refs_2_, ...), custom_call_target="tpu_custom_call" | custom-call | flops 2000000000 | bytes 4000000 | tf_op jit(solution)/shard_map/norm_mine/pallas_call | solution.py:75
  34.2 3.3 %collective-permute-start.3 = (bf16[512,1280]{1,0:T(8,128)(2,1)S(1)}, bf16[512,1280]{1,0:T(8,128)(2,1)}, u32[]{:S(2)}, u32[]{:S(2)}) collective-permute-start(bf16[512,1280]{1,0:T(8,128)(2,1)S(1)} %get-tuple-element.20), channel_id=1, source_target_pairs={{0,1},{1,0},{2,3},{3,2},{4,5},{5,4},{6,7},{7,6},{8,9},{9,8},{10,11... | collective-permute-start | bytes 3932168 | tf_op jit(solution)/shard_map/ppermute | solution.py:20
  38.0 2.2 %collective-permute-start.16 = (bf16[4,40,1280]{2,1,0:T(8,128)(2,1)S(1)}, bf16[4,40,1280]{2,1,0:T(8,128)(2,1)}, u32[]{:S(2)}, u32[]{:S(2)}) collective-permute-start(bf16[4,40,1280]{2,1,0:T(8,128)(2,1)S(1)} %collective-permute-done.15.refs_1_), channel_id=1, source_target_pairs={{0,56},{8,0},{16,8},{24,16},{32,24},{40,32},{48,40},{56,48},{1,57}... | collective-permute-start | bytes 1228808 | tf_op jit(solution)/shard_map/ppermute | solution.py:20
  41.9 2.1 %collective-permute-start.4 = (bf16[320,640]{1,0:T(8,128)(2,1)}, bf16[320,640]{1,0:T(8,128)(2,1)S(1)}, u32[]{:S(2)}, u32[]{:S(2)}) collective-permute-start(bf16[320,640]{1,0:T(8,128)(2,1)} %bitcast.6.w0), channel_id=1, source_target_pairs={{0,192},{64,0},{128,64},{192,128},{1,193},{65,1},{129,65},{193,129... | collective-permute-start | bytes 1228808 | tf_op jit(solution)/shard_map/ppermute | solution.py:20
  44.0 3.9 %collective-permute-done.16.refs_2_ = bf16[4,40,1280]{2,1,0:T(8,128)(2,1)} collective-permute-done((bf16[4,40,1280]{2,1,0:T(8,128)(2,1)S(1)}, bf16[4,40,1280]{2,1,0:T(8,128)(2,1)}, u32[]{:S(2)}, u32[]{:S(2)}) %collective-permute-start.16) | collective-permute-done | bytes 409632 | tf_op jit(solution)/shard_map/ppermute | solution.py:20
  47.8 2.6 %collective-permute-start.17 = (bf16[4,40,1280]{2,1,0:T(8,128)(2,1)}, bf16[4,40,1280]{2,1,0:T(8,128)(2,1)}, u32[]{:S(2)}, u32[]{:S(2)}) collective-permute-start(bf16[4,40,1280]{2,1,0:T(8,128)(2,1)} %collective-permute-done.16.refs_2_), channel_id=1, source_target_pairs={{0,56},{8,0},{16,8},{24,16},{32,24},{40,32},{48,40},{56,48},{1,57}... | collective-permute-start | bytes 1228808 | tf_op jit(solution)/shard_map/ppermute | solution.py:20
  52.2 2.5 %collective-permute-start.5 = (bf16[320,640]{1,0:T(8,128)(2,1)}, bf16[320,640]{1,0:T(8,128)(2,1)}, u32[]{:S(2)}, u32[]{:S(2)}) collective-permute-start(bf16[320,640]{1,0:T(8,128)(2,1)} %bitcast.6.w0), channel_id=1, source_target_pairs={{0,128},{64,192},{128,0},{192,64},{1,129},{65,193},{129,1},{193,65... | collective-permute-start | bytes 1228808 | tf_op jit(solution)/shard_map/ppermute | solution.py:20
  55.6 2.3 %collective-permute-done.17.refs_3_ = bf16[4,40,1280]{2,1,0:T(8,128)(2,1)} collective-permute-done((bf16[4,40,1280]{2,1,0:T(8,128)(2,1)}, bf16[4,40,1280]{2,1,0:T(8,128)(2,1)}, u32[]{:S(2)}, u32[]{:S(2)}) %collective-permute-start.17) | collective-permute-done | bytes 409632 | tf_op jit(solution)/shard_map/ppermute | solution.py:20
  57.9 2.2 %collective-permute-start.18 = (bf16[4,40,1280]{2,1,0:T(8,128)(2,1)}, bf16[4,40,1280]{2,1,0:T(8,128)(2,1)}, u32[]{:S(2)}, u32[]{:S(2)}) collective-permute-start(bf16[4,40,1280]{2,1,0:T(8,128)(2,1)} %collective-permute-done.17.refs_3_), channel_id=1, source_target_pairs={{0,56},{8,0},{16,8},{24,16},{32,24},{40,32},{48,40},{56,48},{1,57}... | collective-permute-start | bytes 1228808 | tf_op jit(solution)/shard_map/ppermute | solution.py:20
  61.9 12.0 %collective-permute-done.6.w3 = bf16[320,640]{1,0:T(8,128)(2,1)} collective-permute-done((bf16[320,640]{1,0:T(8,128)(2,1)}, bf16[320,640]{1,0:T(8,128)(2,1)}, u32[]{:S(2)}, u32[]{:S(2)}) %collective-permute-start.6) | collective-permute-done | bytes 409632 | tf_op jit(solution)/shard_map/ppermute | solution.py:20
  74.9 1.8 %proj_weights.1.w_kept = bf16[1280,256]{1,0:T(8,128)(2,1)S(1)} custom-call(s32[1]{0:T(128)} %bitcast.y_ref, bf16[320,640]{1,0:T(8,128)(2,1)} %bitcast.6.w0, bf16[320,640]{1,0:T(8,128)(2,1)S(1)} %copy-done.6, bf16[320,640]{1,0:T(8,128)(2,1)} %collective-permute-done.5.w2, bf16[320,640]{1,0:T(8,128)(2,1)} %collective-permute-done.6.w3), custom_call_target="tpu_custom_call" | custom-call | flops 1000000000 | bytes 3000000 | tf_op jit(solution)/shard_map/proj_weights/pallas_call | solution.py:193
  77.6 3.1 %norm_other.1.xb_ref = bf16[512,1280]{1,0:T(8,128)(2,1)S(1)} custom-call(f32[1,1280]{1,0:T(1,128)S(1)} %broadcast_in_dim.98.gain_ref, bf16[512,1280]{1,0:T(8,128)(2,1)} %collective-permute-done.3.block), custom_call_target="tpu_custom_call" | custom-call | flops 2000000000 | bytes 3000000 | tf_op jit(solution)/shard_map/norm_other/pallas_call | solution.py:87
  80.8 2.1 %mlp_weights.1 = (bf16[32,40,640]{2,1,0:T(8,128)(2,1)S(1)}, bf16[32,40,640]{2,1,0:T(8,128)(2,1)S(1)}) custom-call(s32[2]{0:T(128)S(1)} %pad_add_fusion.1.yz_ref, bf16[4,40,1280]{2,1,0:T(8,128)(2,1)S(1)} %copy-done.2, bf16[4,40,1280]{2,1,0:T(8,128)(2,1)S(1)} %copy-done.4, bf16[4,40,1280]{2,1,0:T(8,128)(2,1)} %collective-permute-done.16.refs_2_, ...), custom_call_target="tpu_custom_call" | custom-call | flops 1000000000 | bytes 6000000 | tf_op jit(solution)/shard_map/mlp_weights/pallas_call | solution.py:258
  83.5 7.9 %attention.1 = (bf16[512,256]{1,0:T(8,128)(2,1)S(1)}, bf16[512,256]{1,0:T(8,128)(2,1)S(1)}) custom-call(s32[1]{0:T(128)} %bitcast.y_ref, bf16[512,1280]{1,0:T(8,128)(2,1)S(1)} %copy-done.10, bf16[512,1280]{1,0:T(8,128)(2,1)S(1)} %norm_other.1.xb_ref, bf16[320,640]{1,0:T(8,128)(2,1)} %bitcast.6.w0, bf16[320,640]{1,0:T(8,128)(2,1)S(1)} %copy-done.7, ...), custom_call_target="tpu_custom_call" | custom-call | flops 8000000000 | bytes 8000000 | tf_op jit(solution)/shard_map/attention/pallas_call | solution.py:155
  94.5 2.0 %collective-permute-start.10 = (bf16[128,1280]{1,0:T(8,128)(2,1)S(1)}, bf16[128,1280]{1,0:T(8,128)(2,1)S(1)}, u32[]{:S(2)}, u32[]{:S(2)}) collective-permute-start(bf16[128,1280]{1,0:T(8,128)(2,1)S(1)} %get-tuple-element.25), channel_id=1, source_target_pairs={{0,4},{2,6},{4,0},{6,2},{1,5},{3,7},{5,1},{7,3},{8,12},{10,14},{12... | collective-permute-start | bytes 983048 | tf_op jit(solution)/shard_map/ppermute | solution.py:20
  98.0 7.0 %collective-permute-done.10.b = bf16[128,1280]{1,0:T(8,128)(2,1)S(1)} collective-permute-done((bf16[128,1280]{1,0:T(8,128)(2,1)S(1)}, bf16[128,1280]{1,0:T(8,128)(2,1)S(1)}, u32[]{:S(2)}, u32[]{:S(2)}) %collective-permute-start.10) | collective-permute-done | bytes 327712 | tf_op jit(solution)/shard_map/ppermute | solution.py:20
  105.0 4.7 %collective-permute-done.11.d = bf16[128,1280]{1,0:T(8,128)(2,1)S(1)} collective-permute-done((bf16[128,1280]{1,0:T(8,128)(2,1)S(1)}, bf16[128,1280]{1,0:T(8,128)(2,1)S(1)}, u32[]{:S(2)}, u32[]{:S(2)}) %collective-permute-start.11) | collective-permute-done | bytes 327712 | tf_op jit(solution)/shard_map/ppermute | solution.py:20
  109.7 3.1 %collective-permute-done.9.a = bf16[128,1280]{1,0:T(8,128)(2,1)S(1)} collective-permute-done((bf16[128,1280]{1,0:T(8,128)(2,1)S(1)}, bf16[128,1280]{1,0:T(8,128)(2,1)S(1)}, u32[]{:S(2)}, u32[]{:S(2)}) %collective-permute-start.9) | collective-permute-done | bytes 327712 | tf_op jit(solution)/shard_map/ppermute | solution.py:20
  116.6 1.9 %collective-permute-start.29 = (bf16[128,1280]{1,0:T(8,128)(2,1)S(1)}, bf16[128,1280]{1,0:T(8,128)(2,1)S(1)}, u32[]{:S(2)}, u32[]{:S(2)}) collective-permute-start(bf16[128,1280]{1,0:T(8,128)(2,1)S(1)} %get-tuple-element.28.refs_0_), channel_id=1, source_target_pairs={{0,4},{2,6},{4,0},{6,2},{1,5},{3,7},{5,1},{7,3},{8,12},{10,14},{12... | collective-permute-start | bytes 983048 | tf_op jit(solution)/shard_map/ppermute | solution.py:20
  118.5 3.5 %collective-permute-done.25.refs_0_ = bf16[128,1280]{1,0:T(8,128)(2,1)S(1)} collective-permute-done((bf16[128,1280]{1,0:T(8,128)(2,1)S(1)}, bf16[128,1280]{1,0:T(8,128)(2,1)S(1)}, u32[]{:S(2)}, u32[]{:S(2)}) %collective-permute-start.25) | collective-permute-done | bytes 327712 | tf_op jit(solution)/shard_map/ppermute | solution.py:20
  122.8 2.6 %shard_map.119 = (bf16[128,1280]{1,0:T(8,128)(2,1)S(1)}, bf16[128,1280]{1,0:T(8,128)(2,1)S(1)}) custom-call(bf16[128,1280]{1,0:T(8,128)(2,1)S(1)} %collective-permute-done.25.refs_0_, bf16[128,1280]{1,0:T(8,128)(2,1)S(1)} %collective-permute-done.26.refs_1_, bf16[1280,640]{1,0:T(8,128)(2,1)S(1)} %bitcast.41, ...), custom_call_target="tpu_custom_call" | custom-call | flops 3000000000 | bytes 8000000 | tf_op jit(solution)/shard_map/pallas_call | solution.py:286
  125.9 2.3 %collective-permute-start.28 = (bf16[128,1280]{1,0:T(8,128)(2,1)S(1)}, bf16[128,1280]{1,0:T(8,128)(2,1)S(1)}, u32[]{:S(2)}, u32[]{:S(2)}) collective-permute-start(bf16[128,1280]{1,0:T(8,128)(2,1)S(1)} %get-tuple-element.32), channel_id=1, source_target_pairs={{0,6},{2,0},{4,2},{6,4},{1,7},{3,1},{5,3},{7,5},{8,14},{10,8},{12,... | collective-permute-start | bytes 983048 | tf_op jit(solution)/shard_map/ppermute | solution.py:20
  128.2 2.5 %collective-permute-done.29.refs_0_ = bf16[128,1280]{1,0:T(8,128)(2,1)S(1)} collective-permute-done((bf16[128,1280]{1,0:T(8,128)(2,1)S(1)}, bf16[128,1280]{1,0:T(8,128)(2,1)S(1)}, u32[]{:S(2)}, u32[]{:S(2)}) %collective-permute-start.29) | collective-permute-done | bytes 327712 | tf_op jit(solution)/shard_map/ppermute | solution.py:20
  130.7 1.9 %shard_map.120 = bf16[128,1280]{1,0:T(8,128)(2,1)S(1)} custom-call(bf16[128,1280]{1,0:T(8,128)(2,1)S(1)} %collective-permute-done.29.refs_0_, bf16[1280,640]{1,0:T(8,128)(2,1)S(1)} %bitcast.42, bf16[1280,640]{1,0:T(8,128)(2,1)S(1)} %collective-permute-done.22.refs_2_.refs_3_, bf16[1280,640]{1,0:T(8,128)(2,1)S(1)} %bitcast.46, ...), custom_call_target="tpu_custom_call" | custom-call | flops 1500000000 | bytes 8000000 | tf_op jit(solution)/shard_map/pallas_call | solution.py:286
  133.8 1.9 %shard_map.118 = f32[128,1280]{1,0:T(8,128)S(1)} custom-call(bf16[128,1280]{1,0:T(8,128)(2,1)S(1)} %get-tuple-element.28.refs_0_, bf16[1280,640]{1,0:T(8,128)(2,1)S(1)} %bitcast.43, bf16[1280,640]{1,0:T(8,128)(2,1)S(1)} %collective-permute-done.22.refs_2_.refs_3_, bf16[1280,640]{1,0:T(8,128)(2,1)S(1)} %bitcast.47, ...), custom_call_target="tpu_custom_call" | custom-call | flops 1500000000 | bytes 8000000 | tf_op jit(solution)/shard_map/pallas_call | solution.py:286
  135.7 2.8 %collective-permute-done.27 = bf16[128,1280]{1,0:T(8,128)(2,1)S(1)} collective-permute-done((bf16[128,1280]{1,0:T(8,128)(2,1)S(1)}, bf16[128,1280]{1,0:T(8,128)(2,1)S(1)}, u32[]{:S(2)}, u32[]{:S(2)}) %collective-permute-start.27) | collective-permute-done | bytes 327712 | tf_op jit(solution)/shard_map/ppermute | solution.py:20
  138.5 6.2 %collective-permute-done.30 = bf16[128,1280]{1,0:T(8,128)(2,1)S(1)} collective-permute-done((bf16[128,1280]{1,0:T(8,128)(2,1)S(1)}, bf16[128,1280]{1,0:T(8,128)(2,1)S(1)}, u32[]{:S(2)}, u32[]{:S(2)}) %collective-permute-start.30) | collective-permute-done | bytes 327712 | tf_op jit(solution)/shard_map/ppermute | solution.py:20
  (101 shorter events, 31.1 us)
Async XLA Ops:
  0.0 27.5 %collective-permute-start = (bf16[128,1280]{1,0:T(8,128)(2,1)}, bf16[128,1280]{1,0:T(8,128)(2,1)S(1)}, u32[]{:S(2)}, u32[]{:S(2)}) collective-permute-start(bf16[128,1280]{1,0:T(8,128)(2,1)} %bitcast.48), channel_id=1, source_target_pairs={{0,6},{2,0},{4,2},{6,4},{1,7},{3,1},{5,3},{7,5},{8,14},{10,8},{12,... | collective-permute-start | bytes 983048 | tf_op jit(solution)/shard_map/ppermute | solution.py:20
  3.3 24.2 %collective-permute-start.1 = (bf16[128,1280]{1,0:T(8,128)(2,1)}, bf16[128,1280]{1,0:T(8,128)(2,1)S(1)}, u32[]{:S(2)}, u32[]{:S(2)}) collective-permute-start(bf16[128,1280]{1,0:T(8,128)(2,1)} %bitcast.49), channel_id=1, source_target_pairs={{0,4},{2,6},{4,0},{6,2},{1,5},{3,7},{5,1},{7,3},{8,12},{10,14},{12... | collective-permute-start | bytes 983048 | tf_op jit(solution)/shard_map/ppermute | solution.py:20
  4.7 19.4 %collective-permute-start.12 = (bf16[40,1280]{1,0:T(8,128)(2,1)S(1)}, bf16[40,1280]{1,0:T(8,128)(2,1)S(1)}, u32[]{:S(2)}, u32[]{:S(2)}) collective-permute-start(bf16[40,1280]{1,0:T(8,128)(2,1)S(1)} %get-tuple-element.36), channel_id=1, source_target_pairs={{0,192},{64,0},{128,64},{192,128},{1,193},{65,1},{129,65},{193,129... | collective-permute-start | bytes 307208 | tf_op jit(solution)/shard_map/ppermute | solution.py:20
  7.5 17.2 %collective-permute-start.13 = (bf16[40,1280]{1,0:T(8,128)(2,1)S(1)}, bf16[40,1280]{1,0:T(8,128)(2,1)S(1)}, u32[]{:S(2)}, u32[]{:S(2)}) collective-permute-start(bf16[40,1280]{1,0:T(8,128)(2,1)S(1)} %get-tuple-element.36), channel_id=1, source_target_pairs={{0,128},{64,192},{128,0},{192,64},{1,129},{65,193},{129,1},{193,65... | collective-permute-start | bytes 307208 | tf_op jit(solution)/shard_map/ppermute | solution.py:20
  7.8 16.8 %collective-permute-start.14 = (bf16[40,1280]{1,0:T(8,128)(2,1)S(1)}, bf16[40,1280]{1,0:T(8,128)(2,1)S(1)}, u32[]{:S(2)}, u32[]{:S(2)}) collective-permute-start(bf16[40,1280]{1,0:T(8,128)(2,1)S(1)} %get-tuple-element.36), channel_id=1, source_target_pairs={{0,64},{64,128},{128,192},{192,0},{1,65},{65,129},{129,193},{193,1... | collective-permute-start | bytes 307208 | tf_op jit(solution)/shard_map/ppermute | solution.py:20
  10.9 31.0 %all-to-all-start = ((bf16[8,40,640]{2,1,0:T(8,128)(2,1)}), bf16[8,40,640]{2,1,0:T(8,128)(2,1)}, u32[]{:S(2)}, u32[]{:S(2)}) async-start(bf16[8,40,640]{2,1,0:T(8,128)(2,1)} %broadcast_in_dim.99), calls=%async_computation | async-start | bytes 819200 | tf_op jit(solution)/shard_map/all_to_all | solution.py:345
  24.0 8.3 %collective-permute-start.2 = (bf16[128,1280]{1,0:T(8,128)(2,1)}, bf16[128,1280]{1,0:T(8,128)(2,1)S(1)}, u32[]{:S(2)}, u32[]{:S(2)}) collective-permute-start(bf16[128,1280]{1,0:T(8,128)(2,1)} %bitcast.50), channel_id=1, source_target_pairs={{0,2},{2,4},{4,6},{6,0},{1,3},{3,5},{5,7},{7,1},{8,10},{10,12},{12... | collective-permute-start | bytes 983048 | tf_op jit(solution)/shard_map/ppermute | solution.py:20
  24.7 13.3 %collective-permute-start.15 = (bf16[4,40,1280]{2,1,0:T(8,128)(2,1)S(1)}, bf16[4,40,1280]{2,1,0:T(8,128)(2,1)S(1)}, u32[]{:S(2)}, u32[]{:S(2)}) collective-permute-start(bf16[4,40,1280]{2,1,0:T(8,128)(2,1)S(1)} %pad_maximum_fusion.refs_0_), channel_id=1, source_target_pairs={{0,56},{8,0},{16,8},{24,16},{32,24},{40,32},{48,40},{56,48},{1,57}... | collective-permute-start | bytes 1228808 | tf_op jit(solution)/shard_map/ppermute | solution.py:20
  27.5 14.4 %collective-permute-start.19 = (bf16[4,40,1280]{2,1,0:T(8,128)(2,1)S(1)}, bf16[4,40,1280]{2,1,0:T(8,128)(2,1)}, u32[]{:S(2)}, u32[]{:S(2)}) collective-permute-start(bf16[4,40,1280]{2,1,0:T(8,128)(2,1)S(1)} %pad_maximum_fusion.refs_0_), channel_id=1, source_target_pairs={{0,8},{8,16},{16,24},{24,32},{32,40},{40,48},{48,56},{56,0},{1,9},... | collective-permute-start | bytes 1228808 | tf_op jit(solution)/shard_map/ppermute | solution.py:20
  34.2 43.4 %collective-permute-start.3 = (bf16[512,1280]{1,0:T(8,128)(2,1)S(1)}, bf16[512,1280]{1,0:T(8,128)(2,1)}, u32[]{:S(2)}, u32[]{:S(2)}) collective-permute-start(bf16[512,1280]{1,0:T(8,128)(2,1)S(1)} %get-tuple-element.20), channel_id=1, source_target_pairs={{0,1},{1,0},{2,3},{3,2},{4,5},{5,4},{6,7},{7,6},{8,9},{9,8},{10,11... | collective-permute-start | bytes 3932168 | tf_op jit(solution)/shard_map/ppermute | solution.py:20
  38.0 9.9 %collective-permute-start.16 = (bf16[4,40,1280]{2,1,0:T(8,128)(2,1)S(1)}, bf16[4,40,1280]{2,1,0:T(8,128)(2,1)}, u32[]{:S(2)}, u32[]{:S(2)}) collective-permute-start(bf16[4,40,1280]{2,1,0:T(8,128)(2,1)S(1)} %collective-permute-done.15.refs_1_), channel_id=1, source_target_pairs={{0,56},{8,0},{16,8},{24,16},{32,24},{40,32},{48,40},{56,48},{1,57}... | collective-permute-start | bytes 1228808 | tf_op jit(solution)/shard_map/ppermute | solution.py:20
  41.9 12.8 %collective-permute-start.20 = (bf16[4,40,1280]{2,1,0:T(8,128)(2,1)}, bf16[4,40,1280]{2,1,0:T(8,128)(2,1)}, u32[]{:S(2)}, u32[]{:S(2)}) collective-permute-start(bf16[4,40,1280]{2,1,0:T(8,128)(2,1)} %collective-permute-done.19.refs_7_), channel_id=1, source_target_pairs={{0,8},{8,16},{16,24},{24,32},{32,40},{40,48},{48,56},{56,0},{1,9},... | collective-permute-start | bytes 1228808 | tf_op jit(solution)/shard_map/ppermute | solution.py:20
  41.9 12.9 %collective-permute-start.4 = (bf16[320,640]{1,0:T(8,128)(2,1)}, bf16[320,640]{1,0:T(8,128)(2,1)S(1)}, u32[]{:S(2)}, u32[]{:S(2)}) collective-permute-start(bf16[320,640]{1,0:T(8,128)(2,1)} %bitcast.6.w0), channel_id=1, source_target_pairs={{0,192},{64,0},{128,64},{192,128},{1,193},{65,1},{129,65},{193,129... | collective-permute-start | bytes 1228808 | tf_op jit(solution)/shard_map/ppermute | solution.py:20
  47.8 10.0 %collective-permute-start.17 = (bf16[4,40,1280]{2,1,0:T(8,128)(2,1)}, bf16[4,40,1280]{2,1,0:T(8,128)(2,1)}, u32[]{:S(2)}, u32[]{:S(2)}) collective-permute-start(bf16[4,40,1280]{2,1,0:T(8,128)(2,1)} %collective-permute-done.16.refs_2_), channel_id=1, source_target_pairs={{0,56},{8,0},{16,8},{24,16},{32,24},{40,32},{48,40},{56,48},{1,57}... | collective-permute-start | bytes 1228808 | tf_op jit(solution)/shard_map/ppermute | solution.py:20
  52.2 9.7 %collective-permute-start.5 = (bf16[320,640]{1,0:T(8,128)(2,1)}, bf16[320,640]{1,0:T(8,128)(2,1)}, u32[]{:S(2)}, u32[]{:S(2)}) collective-permute-start(bf16[320,640]{1,0:T(8,128)(2,1)} %bitcast.6.w0), channel_id=1, source_target_pairs={{0,128},{64,192},{128,0},{192,64},{1,129},{65,193},{129,1},{193,65... | collective-permute-start | bytes 1228808 | tf_op jit(solution)/shard_map/ppermute | solution.py:20
  54.7 19.2 %collective-permute-start.6 = (bf16[320,640]{1,0:T(8,128)(2,1)}, bf16[320,640]{1,0:T(8,128)(2,1)}, u32[]{:S(2)}, u32[]{:S(2)}) collective-permute-start(bf16[320,640]{1,0:T(8,128)(2,1)} %bitcast.6.w0), channel_id=1, source_target_pairs={{0,64},{64,128},{128,192},{192,0},{1,65},{65,129},{129,193},{193,1... | collective-permute-start | bytes 1228808 | tf_op jit(solution)/shard_map/ppermute | solution.py:20
  55.6 25.2 %collective-permute-start.21 = (bf16[4,40,1280]{2,1,0:T(8,128)(2,1)}, bf16[4,40,1280]{2,1,0:T(8,128)(2,1)}, u32[]{:S(2)}, u32[]{:S(2)}) collective-permute-start(bf16[4,40,1280]{2,1,0:T(8,128)(2,1)} %collective-permute-done.20.refs_6_), channel_id=1, source_target_pairs={{0,8},{8,16},{16,24},{24,32},{32,40},{40,48},{48,56},{56,0},{1,9},... | collective-permute-start | bytes 1228808 | tf_op jit(solution)/shard_map/ppermute | solution.py:20
  57.9 22.9 %collective-permute-start.18 = (bf16[4,40,1280]{2,1,0:T(8,128)(2,1)}, bf16[4,40,1280]{2,1,0:T(8,128)(2,1)}, u32[]{:S(2)}, u32[]{:S(2)}) collective-permute-start(bf16[4,40,1280]{2,1,0:T(8,128)(2,1)} %collective-permute-done.17.refs_3_), channel_id=1, source_target_pairs={{0,56},{8,0},{16,8},{24,16},{32,24},{40,32},{48,40},{56,48},{1,57}... | collective-permute-start | bytes 1228808 | tf_op jit(solution)/shard_map/ppermute | solution.py:20
  76.7 16.9 %collective-permute-start.8 = (bf16[1280,256]{1,0:T(8,128)(2,1)S(1)}, bf16[1280,256]{1,0:T(8,128)(2,1)S(1)}, u32[]{:S(2)}, u32[]{:S(2)}) collective-permute-start(bf16[1280,256]{1,0:T(8,128)(2,1)S(1)} %proj_weights.1.w_kept), channel_id=1, source_target_pairs={{0,1},{1,0},{2,3},{3,2},{4,5},{5,4},{6,7},{7,6},{8,9},{9,8},{10,11... | collective-permute-start | bytes 1966088 | tf_op jit(solution)/shard_map/ppermute | solution.py:20
  82.9 39.9 %collective-permute-start.22 = (bf16[1280,640]{1,0:T(8,128)(2,1)S(1)}, bf16[1280,640]{1,0:T(8,128)(2,1)S(1)}, u32[]{:S(2)}, u32[]{:S(2)}) collective-permute-start(bf16[1280,640]{1,0:T(8,128)(2,1)S(1)} %bitcast.40), channel_id=1, source_target_pairs={{0,1},{1,0},{2,3},{3,2},{4,5},{5,4},{6,7},{7,6},{8,9},{9,8},{10,11... | collective-permute-start | bytes 4915208 | tf_op jit(solution)/shard_map/ppermute | solution.py:20
  83.1 39.7 %collective-permute-start.23 = (bf16[1280,640]{1,0:T(8,128)(2,1)S(1)}, bf16[1280,640]{1,0:T(8,128)(2,1)S(1)}, u32[]{:S(2)}, u32[]{:S(2)}) collective-permute-start(bf16[1280,640]{1,0:T(8,128)(2,1)S(1)} %bitcast.44), channel_id=1, source_target_pairs={{0,1},{1,0},{2,3},{3,2},{4,5},{5,4},{6,7},{7,6},{8,9},{9,8},{10,11... | collective-permute-start | bytes 4915208 | tf_op jit(solution)/shard_map/ppermute | solution.py:20
  91.4 2.2 %collective-permute-start.7 = (bf16[512,256]{1,0:T(8,128)(2,1)S(1)}, bf16[512,256]{1,0:T(8,128)(2,1)S(1)}, u32[]{:S(2)}, u32[]{:S(2)}) collective-permute-start(bf16[512,256]{1,0:T(8,128)(2,1)S(1)} %get-tuple-element.22), channel_id=1, source_target_pairs={{0,1},{1,0},{2,3},{3,2},{4,5},{5,4},{6,7},{7,6},{8,9},{9,8},{10,11... | collective-permute-start | bytes 786440 | tf_op jit(solution)/shard_map/ppermute | solution.py:20
  94.5 10.5 %collective-permute-start.10 = (bf16[128,1280]{1,0:T(8,128)(2,1)S(1)}, bf16[128,1280]{1,0:T(8,128)(2,1)S(1)}, u32[]{:S(2)}, u32[]{:S(2)}) collective-permute-start(bf16[128,1280]{1,0:T(8,128)(2,1)S(1)} %get-tuple-element.25), channel_id=1, source_target_pairs={{0,4},{2,6},{4,0},{6,2},{1,5},{3,7},{5,1},{7,3},{8,12},{10,14},{12... | collective-permute-start | bytes 983048 | tf_op jit(solution)/shard_map/ppermute | solution.py:20
  96.6 13.1 %collective-permute-start.11 = (bf16[128,1280]{1,0:T(8,128)(2,1)S(1)}, bf16[128,1280]{1,0:T(8,128)(2,1)S(1)}, u32[]{:S(2)}, u32[]{:S(2)}) collective-permute-start(bf16[128,1280]{1,0:T(8,128)(2,1)S(1)} %get-tuple-element.26), channel_id=1, source_target_pairs={{0,6},{2,0},{4,2},{6,4},{1,7},{3,1},{5,3},{7,5},{8,14},{10,8},{12,... | collective-permute-start | bytes 983048 | tf_op jit(solution)/shard_map/ppermute | solution.py:20
  97.2 15.6 %collective-permute-start.9 = (bf16[128,1280]{1,0:T(8,128)(2,1)S(1)}, bf16[128,1280]{1,0:T(8,128)(2,1)S(1)}, u32[]{:S(2)}, u32[]{:S(2)}) collective-permute-start(bf16[128,1280]{1,0:T(8,128)(2,1)S(1)} %get-tuple-element.24), channel_id=1, source_target_pairs={{0,2},{2,4},{4,6},{6,0},{1,3},{3,5},{5,7},{7,1},{8,10},{10,12},{12... | collective-permute-start | bytes 983048 | tf_op jit(solution)/shard_map/ppermute | solution.py:20
  113.1 8.9 %collective-permute-start.25 = (bf16[128,1280]{1,0:T(8,128)(2,1)S(1)}, bf16[128,1280]{1,0:T(8,128)(2,1)S(1)}, u32[]{:S(2)}, u32[]{:S(2)}) collective-permute-start(bf16[128,1280]{1,0:T(8,128)(2,1)S(1)} %get-tuple-element.28.refs_0_), channel_id=1, source_target_pairs={{0,6},{2,0},{4,2},{6,4},{1,7},{3,1},{5,3},{7,5},{8,14},{10,8},{12,... | collective-permute-start | bytes 983048 | tf_op jit(solution)/shard_map/ppermute | solution.py:20
  113.3 9.5 %collective-permute-start.26 = (bf16[128,1280]{1,0:T(8,128)(2,1)S(1)}, bf16[128,1280]{1,0:T(8,128)(2,1)S(1)}, u32[]{:S(2)}, u32[]{:S(2)}) collective-permute-start(bf16[128,1280]{1,0:T(8,128)(2,1)S(1)} %get-tuple-element.28.refs_0_), channel_id=1, source_target_pairs={{0,2},{2,4},{4,6},{6,0},{1,3},{3,5},{5,7},{7,1},{8,10},{10,12},{12... | collective-permute-start | bytes 983048 | tf_op jit(solution)/shard_map/ppermute | solution.py:20
  114.7 1.9 %collective-permute-start.24 = (f32[640]{0:T(1024)S(1)}, f32[640]{0:T(1024)S(1)}, u32[]{:S(2)}, u32[]{:S(2)}) collective-permute-start(f32[640]{0:T(1024)S(1)} %copy-done.12), channel_id=1, source_target_pairs={{0,1},{1,0},{2,3},{3,2},{4,5},{5,4},{6,7},{7,6},{8,9},{9,8},{10,11... | collective-permute-start | bytes 7688 | tf_op jit(solution)/shard_map/ppermute | solution.py:20
  116.6 14.1 %collective-permute-start.29 = (bf16[128,1280]{1,0:T(8,128)(2,1)S(1)}, bf16[128,1280]{1,0:T(8,128)(2,1)S(1)}, u32[]{:S(2)}, u32[]{:S(2)}) collective-permute-start(bf16[128,1280]{1,0:T(8,128)(2,1)S(1)} %get-tuple-element.28.refs_0_), channel_id=1, source_target_pairs={{0,4},{2,6},{4,0},{6,2},{1,5},{3,7},{5,1},{7,3},{8,12},{10,14},{12... | collective-permute-start | bytes 983048 | tf_op jit(solution)/shard_map/ppermute | solution.py:20
  125.4 13.1 %collective-permute-start.27 = (bf16[128,1280]{1,0:T(8,128)(2,1)S(1)}, bf16[128,1280]{1,0:T(8,128)(2,1)S(1)}, u32[]{:S(2)}, u32[]{:S(2)}) collective-permute-start(bf16[128,1280]{1,0:T(8,128)(2,1)S(1)} %get-tuple-element.31), channel_id=1, source_target_pairs={{0,2},{2,4},{4,6},{6,0},{1,3},{3,5},{5,7},{7,1},{8,10},{10,12},{12... | collective-permute-start | bytes 983048 | tf_op jit(solution)/shard_map/ppermute | solution.py:20
  125.9 12.6 %collective-permute-start.28 = (bf16[128,1280]{1,0:T(8,128)(2,1)S(1)}, bf16[128,1280]{1,0:T(8,128)(2,1)S(1)}, u32[]{:S(2)}, u32[]{:S(2)}) collective-permute-start(bf16[128,1280]{1,0:T(8,128)(2,1)S(1)} %get-tuple-element.32), channel_id=1, source_target_pairs={{0,6},{2,0},{4,2},{6,4},{1,7},{3,1},{5,3},{7,5},{8,14},{10,8},{12,... | collective-permute-start | bytes 983048 | tf_op jit(solution)/shard_map/ppermute | solution.py:20
  132.6 12.1 %collective-permute-start.30 = (bf16[128,1280]{1,0:T(8,128)(2,1)S(1)}, bf16[128,1280]{1,0:T(8,128)(2,1)S(1)}, u32[]{:S(2)}, u32[]{:S(2)}) collective-permute-start(bf16[128,1280]{1,0:T(8,128)(2,1)S(1)} %shard_map.120), channel_id=1, source_target_pairs={{0,4},{2,6},{4,0},{6,2},{1,5},{3,7},{5,1},{7,3},{8,12},{10,14},{12... | collective-permute-start | bytes 983048 | tf_op jit(solution)/shard_map/ppermute | solution.py:20
  (13 other events, 103.1 us)
where the time goes:
time: 147 us; the launch traced here: 146 us
  waiting for transfers between devices  55.4 us (38%)
  starting transfers between devices  47.9 us (33%)
  Pallas kernels  24.4 us (17%)
  other arithmetic  9.19 us (6%)
  local copies, waits for them, and re-layouts  6.41 us (4%)
  matrix products  1.99 us (1%)
    ppermute x31, waiting for transfers between devices, shift(): return lax.ppermute(x, axis, [(i, (i + by) % n) for i in range(n)])  55.4 us
    ppermute x31, starting transfers between devices, shift(): return lax.ppermute(x, axis, [(i, (i + by) % n) for i in range(n)])  39.7 us
    all_to_all x1, starting transfers between devices, shards(): lax.all_to_all(jnp.broadcast_to(qkvp, (zs, *qkvp.shape)), 'z', 0, 0, tile...  8.19 us
    pallas_call x1, Pallas kernels, attention(): pl.pallas_call(functools.partial(attention_kernel, hs), out_shape=[jax.Sh...  7.89 us
    pallas_call x3, Pallas kernels, mlp(): pl.pallas_call(functools.partial(mlp_kernel, n), out_shape=[jax.ShapeDtyp...  6.46 us
    pallas_call x1, Pallas kernels, norm_other(): pl.pallas_call(norm_other_kernel, out_shape=jax.ShapeDtypeStruct(block.sh...  3.15 us
  transfers between devices with their start and end apart: 32, of which 15 were waited for; matrix products, arithmetic and copies ran while one was open for 10% of the time, Pallas kernels for 17%

commit v1 on v0

--- a/solution.py
+++ b/solution.py
@@ -268,9 +268,10 @@
 
 def mlp_kernel(n, *refs):
     ins, (up_a, up_b, down_a, down_b, bias_a, bias_b) = refs[:n], refs[n : n + 6]
-    outs, (rows, hidden) = refs[n + 6 : 2 * n + 6], refs[2 * n + 6 :]
+    *outs, rows, hidden = refs[n + 6 :]
+    size = ins[0].shape[0]
     for k, r in enumerate(ins):
-        rows[128 * k : 128 * k + 128, :] = r[...]
+        rows[size * k : size * (k + 1), :] = r[...]
     half = up_a.shape[1]
     for i, (up, bias) in enumerate(((up_a, bias_a), (up_b, bias_b))):
         h = jax.nn.gelu(dot(rows[...], up[...]) + bias[...])
@@ -281,19 +282,20 @@
 
 
 def mlp(rows, ups, downs, biases, kind):
-    shape = rows[0].shape
+    total, width = sum(r.shape[0] for r in rows), rows[0].shape[1]
     n = len(rows)
+    blocks = total // 128
     return pl.pallas_call(
         functools.partial(mlp_kernel, n),
-        out_shape=[jax.ShapeDtypeStruct(shape, kind)] * n,
+        out_shape=[jax.ShapeDtypeStruct((128, width), kind)] * blocks,
         in_specs=whole(n + 6),
-        out_specs=whole(n),
+        out_specs=whole(blocks),
         scratch_shapes=[
-            pltpu.VMEM((n * shape[0], shape[1]), BF),
-            pltpu.VMEM((n * shape[0], 2 * ups[0].shape[1]), BF),
+            pltpu.VMEM((total, width), BF),
+            pltpu.VMEM((total, 2 * ups[0].shape[1]), BF),
         ],
         compiler_params=params(24),
-        cost_estimate=cost(1.5e9 * n, 8e6),
+        cost_estimate=cost(1.5e9 * blocks, 8e6),
     )(*rows, *ups, *downs, *(b[None] for b in biases))
 
 
@@ -371,10 +373,11 @@
     mine, *sent = projection(kept_rows, other_rows, proj, proj_other, base)
     received = [shift(sent[k], "x", k + 1) for k in range(3)]
     merged, normed2 = merged_norm(ln2_gain[None], mine, received)
-    rows = [shift(normed2, "x", -k) for k in (1, 2, 3)]
+    ahead, behind = shift(normed2, "x", -1), shift(normed2, "x", 1)
+    far = [shift(ahead[:64], "x", -1), shift(behind[64:], "x", 1)]
     (mine,) = mlp([normed2], ups, downs, biases, F32)
-    first, third = mlp([rows[0], rows[2]], ups, downs, biases, BF)
-    (second,) = mlp([rows[1]], ups, downs, biases, BF)
+    first, third = mlp([ahead, behind], ups, downs, biases, BF)
+    (second,) = mlp(far, ups, downs, biases, BF)
     received = [shift(b, "x", k).astype(F32) for k, b in ((1, first), (3, third), (2, second))]
     out = merged + mine + received[0] + received[1] + received[2]
     return out[:kept].astype(BF)[None]

time: 147 us -> 146 us (level)
  waiting for transfers between devices: 55.4 us -> 53.7 us
    ppermute x31 -> x32, waiting for transfers between devices: 55.4 us -> 53.7 us  [shift(): return lax.ppermute(x, axis, [(i, (i + by) % n) for i in range(n)])]
    ppermute x31 -> x32, starting transfers between devices: 39.7 us -> 39 us  [shift(): return lax.ppermute(x, axis, [(i, (i + by) % n) for i in range(n)])]
  transfers between devices with their start and end apart: 32 -> 33, of which waited for: 15 -> 13; matrix products, arithmetic and copies ran while one was open for 10% -> 10% of each run, Pallas kernels for 17% -> 17%
where the time goes in v1:
time: 146 us; the launch traced here: 143 us
  waiting for transfers between devices  53.7 us (37%)
  starting transfers between devices  47.2 us (32%)
  Pallas kernels  24.4 us (17%)
  other arithmetic  9.16 us (6%)
  local copies, waits for them, and re-layouts  6.45 us (4%)
  matrix products  1.99 us (1%)
    ppermute x32, waiting for transfers between devices, shift(): return lax.ppermute(x, axis, [(i, (i + by) % n) for i in range(n)])  53.7 us
    ppermute x32, starting transfers between devices, shift(): return lax.ppermute(x, axis, [(i, (i + by) % n) for i in range(n)])  39 us
    all_to_all x1, starting transfers between devices, shards(): lax.all_to_all(jnp.broadcast_to(qkvp, (zs, *qkvp.shape)), 'z', 0, 0, tile...  8.19 us
    pallas_call x1, Pallas kernels, attention(): pl.pallas_call(functools.partial(attention_kernel, hs), out_shape=[jax.Sh...  7.89 us
    pallas_call x3, Pallas kernels, mlp(): pl.pallas_call(functools.partial(mlp_kernel, n), out_shape=[jax.ShapeDtyp...  6.45 us
    pallas_call x1, Pallas kernels, norm_other(): pl.pallas_call(norm_other_kernel, out_shape=jax.ShapeDtypeStruct(block.sh...  3.15 us
  transfers between devices with their start and end apart: 33, of which 13 were waited for; matrix products, arithmetic and copies ran while one was open for 10% of the time, Pallas kernels for 17%

profile of v1, /device:TPU:1, one launch (start us, length us, event | category | flops | bytes accessed | tf_op | source)
XLA Modules:
  0.0 143.3 jit_solution(9173605707234392027)
XLA Ops:
  0.0 3.3 %collective-permute-start = (bf16[128,1280]{1,0:T(8,128)(2,1)}, bf16[128,1280]{1,0:T(8,128)(2,1)S(1)}, u32[]{:S(2)}, u32[]{:S(2)}) collective-permute-start(bf16[128,1280]{1,0:T(8,128)(2,1)} %bitcast.48), channel_id=1, source_target_pairs={{0,6},{2,0},{4,2},{6,4},{1,7},{3,1},{5,3},{7,5},{8,14},{10,8},{12,... | collective-permute-start | bytes 983048 | tf_op jit(solution)/shard_map/ppermute | solution.py:20
  4.7 2.8 %collective-permute-start.12 = (bf16[40,1280]{1,0:T(8,128)(2,1)S(1)}, bf16[40,1280]{1,0:T(8,128)(2,1)S(1)}, u32[]{:S(2)}, u32[]{:S(2)}) collective-permute-start(bf16[40,1280]{1,0:T(8,128)(2,1)S(1)} %get-tuple-element.36), channel_id=1, source_target_pairs={{0,192},{64,0},{128,64},{192,128},{1,193},{65,1},{129,65},{193,129... | collective-permute-start | bytes 307208 | tf_op jit(solution)/shard_map/ppermute | solution.py:20
  10.9 8.2 %all-to-all-start = ((bf16[8,40,640]{2,1,0:T(8,128)(2,1)}), bf16[8,40,640]{2,1,0:T(8,128)(2,1)}, u32[]{:S(2)}, u32[]{:S(2)}) async-start(bf16[8,40,640]{2,1,0:T(8,128)(2,1)} %broadcast_in_dim.99), calls=%async_computation | async-start | bytes 819200 | tf_op jit(solution)/shard_map/all_to_all | solution.py:347
  24.7 2.8 %collective-permute-start.15 = (bf16[4,40,1280]{2,1,0:T(8,128)(2,1)S(1)}, bf16[4,40,1280]{2,1,0:T(8,128)(2,1)S(1)}, u32[]{:S(2)}, u32[]{:S(2)}) collective-permute-start(bf16[4,40,1280]{2,1,0:T(8,128)(2,1)S(1)} %pad_maximum_fusion.refs_0_), channel_id=1, source_target_pairs={{0,56},{8,0},{16,8},{24,16},{32,24},{40,32},{48,40},{56,48},{1,57}... | collective-permute-start | bytes 1228808 | tf_op jit(solution)/shard_map/ppermute | solution.py:20
  27.5 4.9 %collective-permute-done.2.refs_3_ = bf16[128,1280]{1,0:T(8,128)(2,1)S(1)} collective-permute-done((bf16[128,1280]{1,0:T(8,128)(2,1)}, bf16[128,1280]{1,0:T(8,128)(2,1)S(1)}, u32[]{:S(2)}, u32[]{:S(2)}) %collective-permute-start.2) | collective-permute-done | bytes 327712 | tf_op jit(solution)/shard_map/ppermute | solution.py:20
  32.4 1.8 %norm_mine.1 = (bf16[512,1280]{1,0:T(8,128)(2,1)S(1)}, bf16[512,1280]{1,0:T(8,128)(2,1)S(1)}) custom-call(f32[1,1280]{1,0:T(1,128)S(1)} %broadcast_in_dim.98.gain_ref, bf16[128,1280]{1,0:T(8,128)(2,1)S(1)} %bitcast.51, bf16[128,1280]{1,0:T(8,128)(2,1)S(1)} %collective-permute-done.refs_1_, bf16[128,1280]{1,0:T(8,128)(2,1)S(1)} %collective-permute-done.1.refs_2_, ...), custom_call_target="tpu_custom_call" | custom-call | flops 2000000000 | bytes 4000000 | tf_op jit(solution)/shard_map/norm_mine/pallas_call | solution.py:75
  34.3 3.3 %collective-permute-start.3 = (bf16[512,1280]{1,0:T(8,128)(2,1)S(1)}, bf16[512,1280]{1,0:T(8,128)(2,1)}, u32[]{:S(2)}, u32[]{:S(2)}) collective-permute-start(bf16[512,1280]{1,0:T(8,128)(2,1)S(1)} %get-tuple-element.20), channel_id=1, source_target_pairs={{0,1},{1,0},{2,3},{3,2},{4,5},{5,4},{6,7},{7,6},{8,9},{9,8},{10,11... | collective-permute-start | bytes 3932168 | tf_op jit(solution)/shard_map/ppermute | solution.py:20
  38.0 2.2 %collective-permute-start.16 = (bf16[4,40,1280]{2,1,0:T(8,128)(2,1)S(1)}, bf16[4,40,1280]{2,1,0:T(8,128)(2,1)}, u32[]{:S(2)}, u32[]{:S(2)}) collective-permute-start(bf16[4,40,1280]{2,1,0:T(8,128)(2,1)S(1)} %collective-permute-done.15.refs_1_), channel_id=1, source_target_pairs={{0,56},{8,0},{16,8},{24,16},{32,24},{40,32},{48,40},{56,48},{1,57}... | collective-permute-start | bytes 1228808 | tf_op jit(solution)/shard_map/ppermute | solution.py:20
  40.2 1.7 %fusion = bf16[2,512,1024]{2,1,0:T(8,128)(2,1)} fusion(f32[2,512]{1,0:T(2,128)S(1)} %compare_select_fusion, f32[1024]{0:T(1024)S(1)} %get-tuple-element.44, s32[1024]{0:T(1024)S(1)} %pad_add_fusion, s32[2,512]{1,0:T(2,128)S(1)} %add_bitcast_fusion), kind=kLoop, calls=%fused_computation.2 | loop fusion | flops 4194304 | bytes 2113536 | tf_op jit(solution)/shard_map/convert_element_type | solution.py:321
  41.9 2.1 %collective-permute-start.4 = (bf16[320,640]{1,0:T(8,128)(2,1)}, bf16[320,640]{1,0:T(8,128)(2,1)S(1)}, u32[]{:S(2)}, u32[]{:S(2)}) collective-permute-start(bf16[320,640]{1,0:T(8,128)(2,1)} %bitcast.6.w0), channel_id=1, source_target_pairs={{0,192},{64,0},{128,64},{192,128},{1,193},{65,1},{129,65},{193,129... | collective-permute-start | bytes 1228808 | tf_op jit(solution)/shard_map/ppermute | solution.py:20
  44.0 3.9 %collective-permute-done.16.refs_2_ = bf16[4,40,1280]{2,1,0:T(8,128)(2,1)} collective-permute-done((bf16[4,40,1280]{2,1,0:T(8,128)(2,1)S(1)}, bf16[4,40,1280]{2,1,0:T(8,128)(2,1)}, u32[]{:S(2)}, u32[]{:S(2)}) %collective-permute-start.16) | collective-permute-done | bytes 409632 | tf_op jit(solution)/shard_map/ppermute | solution.py:20
  47.9 2.6 %collective-permute-start.17 = (bf16[4,40,1280]{2,1,0:T(8,128)(2,1)}, bf16[4,40,1280]{2,1,0:T(8,128)(2,1)}, u32[]{:S(2)}, u32[]{:S(2)}) collective-permute-start(bf16[4,40,1280]{2,1,0:T(8,128)(2,1)} %collective-permute-done.16.refs_2_), channel_id=1, source_target_pairs={{0,56},{8,0},{16,8},{24,16},{32,24},{40,32},{48,40},{56,48},{1,57}... | collective-permute-start | bytes 1228808 | tf_op jit(solution)/shard_map/ppermute | solution.py:20
  50.5 1.7 %slice_bitcast_fusion = (bf16[512,1024]{1,0:T(8,128)(2,1)S(1)}, bf16[512,1024]{1,0:T(8,128)(2,1)S(1)}) fusion(bf16[2,512,1024]{2,1,0:T(8,128)(2,1)} %fusion), kind=kLoop, calls=%fused_computation.4 | loop fusion | bytes 4194304 | tf_op jit(solution)/shard_map/squeeze | solution.py:328
  52.2 2.5 %collective-permute-start.5 = (bf16[320,640]{1,0:T(8,128)(2,1)}, bf16[320,640]{1,0:T(8,128)(2,1)}, u32[]{:S(2)}, u32[]{:S(2)}) collective-permute-start(bf16[320,640]{1,0:T(8,128)(2,1)} %bitcast.6.w0), channel_id=1, source_target_pairs={{0,128},{64,192},{128,0},{192,64},{1,129},{65,193},{129,1},{193,65... | collective-permute-start | bytes 1228808 | tf_op jit(solution)/shard_map/ppermute | solution.py:20
  55.6 2.3 %collective-permute-done.17.refs_3_ = bf16[4,40,1280]{2,1,0:T(8,128)(2,1)} collective-permute-done((bf16[4,40,1280]{2,1,0:T(8,128)(2,1)}, bf16[4,40,1280]{2,1,0:T(8,128)(2,1)}, u32[]{:S(2)}, u32[]{:S(2)}) %collective-permute-start.17) | collective-permute-done | bytes 409632 | tf_op jit(solution)/shard_map/ppermute | solution.py:20
  57.9 2.2 %collective-permute-start.18 = (bf16[4,40,1280]{2,1,0:T(8,128)(2,1)}, bf16[4,40,1280]{2,1,0:T(8,128)(2,1)}, u32[]{:S(2)}, u32[]{:S(2)}) collective-permute-start(bf16[4,40,1280]{2,1,0:T(8,128)(2,1)} %collective-permute-done.17.refs_3_), channel_id=1, source_target_pairs={{0,56},{8,0},{16,8},{24,16},{32,24},{40,32},{48,40},{56,48},{1,57}... | collective-permute-start | bytes 1228808 | tf_op jit(solution)/shard_map/ppermute | solution.py:20
  61.9 12.0 %collective-permute-done.6.w3 = bf16[320,640]{1,0:T(8,128)(2,1)} collective-permute-done((bf16[320,640]{1,0:T(8,128)(2,1)}, bf16[320,640]{1,0:T(8,128)(2,1)}, u32[]{:S(2)}, u32[]{:S(2)}) %collective-permute-start.6) | collective-permute-done | bytes 409632 | tf_op jit(solution)/shard_map/ppermute | solution.py:20
  74.9 1.8 %proj_weights.1.w_kept = bf16[1280,256]{1,0:T(8,128)(2,1)S(1)} custom-call(s32[1]{0:T(128)} %bitcast.y_ref, bf16[320,640]{1,0:T(8,128)(2,1)} %bitcast.6.w0, bf16[320,640]{1,0:T(8,128)(2,1)S(1)} %copy-done.6, bf16[320,640]{1,0:T(8,128)(2,1)} %collective-permute-done.5.w2, bf16[320,640]{1,0:T(8,128)(2,1)} %collective-permute-done.6.w3), custom_call_target="tpu_custom_call" | custom-call | flops 1000000000 | bytes 3000000 | tf_op jit(solution)/shard_map/proj_weights/pallas_call | solution.py:193
  77.6 3.1 %norm_other.1.xb_ref = bf16[512,1280]{1,0:T(8,128)(2,1)S(1)} custom-call(f32[1,1280]{1,0:T(1,128)S(1)} %broadcast_in_dim.98.gain_ref, bf16[512,1280]{1,0:T(8,128)(2,1)} %collective-permute-done.3.block), custom_call_target="tpu_custom_call" | custom-call | flops 2000000000 | bytes 3000000 | tf_op jit(solution)/shard_map/norm_other/pallas_call | solution.py:87
  80.9 2.1 %mlp_weights.1 = (bf16[32,40,640]{2,1,0:T(8,128)(2,1)S(1)}, bf16[32,40,640]{2,1,0:T(8,128)(2,1)S(1)}) custom-call(s32[2]{0:T(128)S(1)} %pad_add_fusion.1.yz_ref, bf16[4,40,1280]{2,1,0:T(8,128)(2,1)S(1)} %copy-done.2, bf16[4,40,1280]{2,1,0:T(8,128)(2,1)S(1)} %copy-done.4, bf16[4,40,1280]{2,1,0:T(8,128)(2,1)} %collective-permute-done.16.refs_2_, ...), custom_call_target="tpu_custom_call" | custom-call | flops 1000000000 | bytes 6000000 | tf_op jit(solution)/shard_map/mlp_weights/pallas_call | solution.py:258
  83.5 7.9 %attention.1 = (bf16[512,256]{1,0:T(8,128)(2,1)S(1)}, bf16[512,256]{1,0:T(8,128)(2,1)S(1)}) custom-call(s32[1]{0:T(128)} %bitcast.y_ref, bf16[512,1280]{1,0:T(8,128)(2,1)S(1)} %copy-done.10, bf16[512,1280]{1,0:T(8,128)(2,1)S(1)} %norm_other.1.xb_ref, bf16[320,640]{1,0:T(8,128)(2,1)} %bitcast.6.w0, bf16[320,640]{1,0:T(8,128)(2,1)S(1)} %copy-done.7, ...), custom_call_target="tpu_custom_call" | custom-call | flops 8000000000 | bytes 8000000 | tf_op jit(solution)/shard_map/attention/pallas_call | solution.py:155
  94.6 2.0 %collective-permute-start.10 = (bf16[128,1280]{1,0:T(8,128)(2,1)S(1)}, bf16[128,1280]{1,0:T(8,128)(2,1)S(1)}, u32[]{:S(2)}, u32[]{:S(2)}) collective-permute-start(bf16[128,1280]{1,0:T(8,128)(2,1)S(1)} %get-tuple-element.25), channel_id=1, source_target_pairs={{0,4},{2,6},{4,0},{6,2},{1,5},{3,7},{5,1},{7,3},{8,12},{10,14},{12... | collective-permute-start | bytes 983048 | tf_op jit(solution)/shard_map/ppermute | solution.py:20
  98.1 7.0 %collective-permute-done.10.b = bf16[128,1280]{1,0:T(8,128)(2,1)S(1)} collective-permute-done((bf16[128,1280]{1,0:T(8,128)(2,1)S(1)}, bf16[128,1280]{1,0:T(8,128)(2,1)S(1)}, u32[]{:S(2)}, u32[]{:S(2)}) %collective-permute-start.10) | collective-permute-done | bytes 327712 | tf_op jit(solution)/shard_map/ppermute | solution.py:20
  105.0 4.7 %collective-permute-done.11.d = bf16[128,1280]{1,0:T(8,128)(2,1)S(1)} collective-permute-done((bf16[128,1280]{1,0:T(8,128)(2,1)S(1)}, bf16[128,1280]{1,0:T(8,128)(2,1)S(1)}, u32[]{:S(2)}, u32[]{:S(2)}) %collective-permute-start.11) | collective-permute-done | bytes 327712 | tf_op jit(solution)/shard_map/ppermute | solution.py:20
  109.7 3.1 %collective-permute-done.9.a = bf16[128,1280]{1,0:T(8,128)(2,1)S(1)} collective-permute-done((bf16[128,1280]{1,0:T(8,128)(2,1)S(1)}, bf16[128,1280]{1,0:T(8,128)(2,1)S(1)}, u32[]{:S(2)}, u32[]{:S(2)}) %collective-permute-start.9) | collective-permute-done | bytes 327712 | tf_op jit(solution)/shard_map/ppermute | solution.py:20
  116.6 5.4 %collective-permute-done.25.refs_0_ = bf16[128,1280]{1,0:T(8,128)(2,1)S(1)} collective-permute-done((bf16[128,1280]{1,0:T(8,128)(2,1)S(1)}, bf16[128,1280]{1,0:T(8,128)(2,1)S(1)}, u32[]{:S(2)}, u32[]{:S(2)}) %collective-permute-start.25) | collective-permute-done | bytes 327712 | tf_op jit(solution)/shard_map/ppermute | solution.py:20
  123.7 2.6 %shard_map.119 = (bf16[128,1280]{1,0:T(8,128)(2,1)S(1)}, bf16[128,1280]{1,0:T(8,128)(2,1)S(1)}) custom-call(bf16[128,1280]{1,0:T(8,128)(2,1)S(1)} %collective-permute-done.25.refs_0_, bf16[128,1280]{1,0:T(8,128)(2,1)S(1)} %collective-permute-done.26.refs_1_, bf16[1280,640]{1,0:T(8,128)(2,1)S(1)} %bitcast.41, ...), custom_call_target="tpu_custom_call" | custom-call | flops 3000000000 | bytes 8000000 | tf_op jit(solution)/shard_map/pallas_call | solution.py:288
  126.6 2.5 %collective-permute-start.28 = (bf16[128,1280]{1,0:T(8,128)(2,1)S(1)}, bf16[128,1280]{1,0:T(8,128)(2,1)S(1)}, u32[]{:S(2)}, u32[]{:S(2)}) collective-permute-start(bf16[128,1280]{1,0:T(8,128)(2,1)S(1)} %get-tuple-element.32), channel_id=1, source_target_pairs={{0,6},{2,0},{4,2},{6,4},{1,7},{3,1},{5,3},{7,5},{8,14},{10,8},{12,... | collective-permute-start | bytes 983048 | tf_op jit(solution)/shard_map/ppermute | solution.py:20
  129.1 1.9 %shard_map.120 = bf16[128,1280]{1,0:T(8,128)(2,1)S(1)} custom-call(bf16[64,1280]{1,0:T(8,128)(2,1)S(1)} %collective-permute-done.29.refs_0_, bf16[64,1280]{1,0:T(8,128)(2,1)S(1)} %collective-permute-done.30.refs_1_, bf16[1280,640]{1,0:T(8,128)(2,1)S(1)} %bitcast.42, bf16[1280,640]{1,0:T(8,128)(2,1)S(1)} %collective-permute-done.22.refs_2_.refs_3_, ...), custom_call_target="tpu_custom_call" | custom-call | flops 1500000000 | bytes 8000000 | tf_op jit(solution)/shard_map/pallas_call | solution.py:288
  131.8 1.9 %shard_map.118 = f32[128,1280]{1,0:T(8,128)S(1)} custom-call(bf16[128,1280]{1,0:T(8,128)(2,1)S(1)} %get-tuple-element.28.refs_0_, bf16[1280,640]{1,0:T(8,128)(2,1)S(1)} %bitcast.43, bf16[1280,640]{1,0:T(8,128)(2,1)S(1)} %collective-permute-done.22.refs_2_.refs_3_, bf16[1280,640]{1,0:T(8,128)(2,1)S(1)} %bitcast.47, ...), custom_call_target="tpu_custom_call" | custom-call | flops 1500000000 | bytes 8000000 | tf_op jit(solution)/shard_map/pallas_call | solution.py:288
  133.7 4.4 %collective-permute-done.27 = bf16[128,1280]{1,0:T(8,128)(2,1)S(1)} collective-permute-done((bf16[128,1280]{1,0:T(8,128)(2,1)S(1)}, bf16[128,1280]{1,0:T(8,128)(2,1)S(1)}, u32[]{:S(2)}, u32[]{:S(2)}) %collective-permute-start.27) | collective-permute-done | bytes 327712 | tf_op jit(solution)/shard_map/ppermute | solution.py:20
  138.2 4.3 %collective-permute-done.31 = bf16[128,1280]{1,0:T(8,128)(2,1)S(1)} collective-permute-done((bf16[128,1280]{1,0:T(8,128)(2,1)S(1)}, bf16[128,1280]{1,0:T(8,128)(2,1)S(1)}, u32[]{:S(2)}, u32[]{:S(2)}) %collective-permute-start.31) | collective-permute-done | bytes 327712 | tf_op jit(solution)/shard_map/ppermute | solution.py:20
  (105 shorter events, 28.0 us)
Async XLA Ops:
  0.0 27.5 %collective-permute-start = (bf16[128,1280]{1,0:T(8,128)(2,1)}, bf16[128,1280]{1,0:T(8,128)(2,1)S(1)}, u32[]{:S(2)}, u32[]{:S(2)}) collective-permute-start(bf16[128,1280]{1,0:T(8,128)(2,1)} %bitcast.48), channel_id=1, source_target_pairs={{0,6},{2,0},{4,2},{6,4},{1,7},{3,1},{5,3},{7,5},{8,14},{10,8},{12,... | collective-permute-start | bytes 983048 | tf_op jit(solution)/shard_map/ppermute | solution.py:20
  3.3 24.2 %collective-permute-start.1 = (bf16[128,1280]{1,0:T(8,128)(2,1)}, bf16[128,1280]{1,0:T(8,128)(2,1)S(1)}, u32[]{:S(2)}, u32[]{:S(2)}) collective-permute-start(bf16[128,1280]{1,0:T(8,128)(2,1)} %bitcast.49), channel_id=1, source_target_pairs={{0,4},{2,6},{4,0},{6,2},{1,5},{3,7},{5,1},{7,3},{8,12},{10,14},{12... | collective-permute-start | bytes 983048 | tf_op jit(solution)/shard_map/ppermute | solution.py:20
  4.7 19.4 %collective-permute-start.12 = (bf16[40,1280]{1,0:T(8,128)(2,1)S(1)}, bf16[40,1280]{1,0:T(8,128)(2,1)S(1)}, u32[]{:S(2)}, u32[]{:S(2)}) collective-permute-start(bf16[40,1280]{1,0:T(8,128)(2,1)S(1)} %get-tuple-element.36), channel_id=1, source_target_pairs={{0,192},{64,0},{128,64},{192,128},{1,193},{65,1},{129,65},{193,129... | collective-permute-start | bytes 307208 | tf_op jit(solution)/shard_map/ppermute | solution.py:20
  7.5 17.2 %collective-permute-start.13 = (bf16[40,1280]{1,0:T(8,128)(2,1)S(1)}, bf16[40,1280]{1,0:T(8,128)(2,1)S(1)}, u32[]{:S(2)}, u32[]{:S(2)}) collective-permute-start(bf16[40,1280]{1,0:T(8,128)(2,1)S(1)} %get-tuple-element.36), channel_id=1, source_target_pairs={{0,128},{64,192},{128,0},{192,64},{1,129},{65,193},{129,1},{193,65... | collective-permute-start | bytes 307208 | tf_op jit(solution)/shard_map/ppermute | solution.py:20
  7.8 16.8 %collective-permute-start.14 = (bf16[40,1280]{1,0:T(8,128)(2,1)S(1)}, bf16[40,1280]{1,0:T(8,128)(2,1)S(1)}, u32[]{:S(2)}, u32[]{:S(2)}) collective-permute-start(bf16[40,1280]{1,0:T(8,128)(2,1)S(1)} %get-tuple-element.36), channel_id=1, source_target_pairs={{0,64},{64,128},{128,192},{192,0},{1,65},{65,129},{129,193},{193,1... | collective-permute-start | bytes 307208 | tf_op jit(solution)/shard_map/ppermute | solution.py:20
  10.9 31.0 %all-to-all-start = ((bf16[8,40,640]{2,1,0:T(8,128)(2,1)}), bf16[8,40,640]{2,1,0:T(8,128)(2,1)}, u32[]{:S(2)}, u32[]{:S(2)}) async-start(bf16[8,40,640]{2,1,0:T(8,128)(2,1)} %broadcast_in_dim.99), calls=%async_computation | async-start | bytes 819200 | tf_op jit(solution)/shard_map/all_to_all | solution.py:347
  24.0 8.3 %collective-permute-start.2 = (bf16[128,1280]{1,0:T(8,128)(2,1)}, bf16[128,1280]{1,0:T(8,128)(2,1)S(1)}, u32[]{:S(2)}, u32[]{:S(2)}) collective-permute-start(bf16[128,1280]{1,0:T(8,128)(2,1)} %bitcast.50), channel_id=1, source_target_pairs={{0,2},{2,4},{4,6},{6,0},{1,3},{3,5},{5,7},{7,1},{8,10},{10,12},{12... | collective-permute-start | bytes 983048 | tf_op jit(solution)/shard_map/ppermute | solution.py:20
  24.7 13.3 %collective-permute-start.15 = (bf16[4,40,1280]{2,1,0:T(8,128)(2,1)S(1)}, bf16[4,40,1280]{2,1,0:T(8,128)(2,1)S(1)}, u32[]{:S(2)}, u32[]{:S(2)}) collective-permute-start(bf16[4,40,1280]{2,1,0:T(8,128)(2,1)S(1)} %pad_maximum_fusion.refs_0_), channel_id=1, source_target_pairs={{0,56},{8,0},{16,8},{24,16},{32,24},{40,32},{48,40},{56,48},{1,57}... | collective-permute-start | bytes 1228808 | tf_op jit(solution)/shard_map/ppermute | solution.py:20
  27.5 14.4 %collective-permute-start.19 = (bf16[4,40,1280]{2,1,0:T(8,128)(2,1)S(1)}, bf16[4,40,1280]{2,1,0:T(8,128)(2,1)}, u32[]{:S(2)}, u32[]{:S(2)}) collective-permute-start(bf16[4,40,1280]{2,1,0:T(8,128)(2,1)S(1)} %pad_maximum_fusion.refs_0_), channel_id=1, source_target_pairs={{0,8},{8,16},{16,24},{24,32},{32,40},{40,48},{48,56},{56,0},{1,9},... | collective-permute-start | bytes 1228808 | tf_op jit(solution)/shard_map/ppermute | solution.py:20
  34.3 43.4 %collective-permute-start.3 = (bf16[512,1280]{1,0:T(8,128)(2,1)S(1)}, bf16[512,1280]{1,0:T(8,128)(2,1)}, u32[]{:S(2)}, u32[]{:S(2)}) collective-permute-start(bf16[512,1280]{1,0:T(8,128)(2,1)S(1)} %get-tuple-element.20), channel_id=1, source_target_pairs={{0,1},{1,0},{2,3},{3,2},{4,5},{5,4},{6,7},{7,6},{8,9},{9,8},{10,11... | collective-permute-start | bytes 3932168 | tf_op jit(solution)/shard_map/ppermute | solution.py:20
  38.0 9.9 %collective-permute-start.16 = (bf16[4,40,1280]{2,1,0:T(8,128)(2,1)S(1)}, bf16[4,40,1280]{2,1,0:T(8,128)(2,1)}, u32[]{:S(2)}, u32[]{:S(2)}) collective-permute-start(bf16[4,40,1280]{2,1,0:T(8,128)(2,1)S(1)} %collective-permute-done.15.refs_1_), channel_id=1, source_target_pairs={{0,56},{8,0},{16,8},{24,16},{32,24},{40,32},{48,40},{56,48},{1,57}... | collective-permute-start | bytes 1228808 | tf_op jit(solution)/shard_map/ppermute | solution.py:20
  41.9 12.8 %collective-permute-start.20 = (bf16[4,40,1280]{2,1,0:T(8,128)(2,1)}, bf16[4,40,1280]{2,1,0:T(8,128)(2,1)}, u32[]{:S(2)}, u32[]{:S(2)}) collective-permute-start(bf16[4,40,1280]{2,1,0:T(8,128)(2,1)} %collective-permute-done.19.refs_7_), channel_id=1, source_target_pairs={{0,8},{8,16},{16,24},{24,32},{32,40},{40,48},{48,56},{56,0},{1,9},... | collective-permute-start | bytes 1228808 | tf_op jit(solution)/shard_map/ppermute | solution.py:20
  41.9 12.9 %collective-permute-start.4 = (bf16[320,640]{1,0:T(8,128)(2,1)}, bf16[320,640]{1,0:T(8,128)(2,1)S(1)}, u32[]{:S(2)}, u32[]{:S(2)}) collective-permute-start(bf16[320,640]{1,0:T(8,128)(2,1)} %bitcast.6.w0), channel_id=1, source_target_pairs={{0,192},{64,0},{128,64},{192,128},{1,193},{65,1},{129,65},{193,129... | collective-permute-start | bytes 1228808 | tf_op jit(solution)/shard_map/ppermute | solution.py:20
  47.9 10.0 %collective-permute-start.17 = (bf16[4,40,1280]{2,1,0:T(8,128)(2,1)}, bf16[4,40,1280]{2,1,0:T(8,128)(2,1)}, u32[]{:S(2)}, u32[]{:S(2)}) collective-permute-start(bf16[4,40,1280]{2,1,0:T(8,128)(2,1)} %collective-permute-done.16.refs_2_), channel_id=1, source_target_pairs={{0,56},{8,0},{16,8},{24,16},{32,24},{40,32},{48,40},{56,48},{1,57}... | collective-permute-start | bytes 1228808 | tf_op jit(solution)/shard_map/ppermute | solution.py:20
  52.2 9.7 %collective-permute-start.5 = (bf16[320,640]{1,0:T(8,128)(2,1)}, bf16[320,640]{1,0:T(8,128)(2,1)}, u32[]{:S(2)}, u32[]{:S(2)}) collective-permute-start(bf16[320,640]{1,0:T(8,128)(2,1)} %bitcast.6.w0), channel_id=1, source_target_pairs={{0,128},{64,192},{128,0},{192,64},{1,129},{65,193},{129,1},{193,65... | collective-permute-start | bytes 1228808 | tf_op jit(solution)/shard_map/ppermute | solution.py:20
  54.7 19.2 %collective-permute-start.6 = (bf16[320,640]{1,0:T(8,128)(2,1)}, bf16[320,640]{1,0:T(8,128)(2,1)}, u32[]{:S(2)}, u32[]{:S(2)}) collective-permute-start(bf16[320,640]{1,0:T(8,128)(2,1)} %bitcast.6.w0), channel_id=1, source_target_pairs={{0,64},{64,128},{128,192},{192,0},{1,65},{65,129},{129,193},{193,1... | collective-permute-start | bytes 1228808 | tf_op jit(solution)/shard_map/ppermute | solution.py:20
  55.6 25.2 %collective-permute-start.21 = (bf16[4,40,1280]{2,1,0:T(8,128)(2,1)}, bf16[4,40,1280]{2,1,0:T(8,128)(2,1)}, u32[]{:S(2)}, u32[]{:S(2)}) collective-permute-start(bf16[4,40,1280]{2,1,0:T(8,128)(2,1)} %collective-permute-done.20.refs_6_), channel_id=1, source_target_pairs={{0,8},{8,16},{16,24},{24,32},{32,40},{40,48},{48,56},{56,0},{1,9},... | collective-permute-start | bytes 1228808 | tf_op jit(solution)/shard_map/ppermute | solution.py:20
  57.9 22.9 %collective-permute-start.18 = (bf16[4,40,1280]{2,1,0:T(8,128)(2,1)}, bf16[4,40,1280]{2,1,0:T(8,128)(2,1)}, u32[]{:S(2)}, u32[]{:S(2)}) collective-permute-start(bf16[4,40,1280]{2,1,0:T(8,128)(2,1)} %collective-permute-done.17.refs_3_), channel_id=1, source_target_pairs={{0,56},{8,0},{16,8},{24,16},{32,24},{40,32},{48,40},{56,48},{1,57}... | collective-permute-start | bytes 1228808 | tf_op jit(solution)/shard_map/ppermute | solution.py:20
  76.7 16.9 %collective-permute-start.8 = (bf16[1280,256]{1,0:T(8,128)(2,1)S(1)}, bf16[1280,256]{1,0:T(8,128)(2,1)S(1)}, u32[]{:S(2)}, u32[]{:S(2)}) collective-permute-start(bf16[1280,256]{1,0:T(8,128)(2,1)S(1)} %proj_weights.1.w_kept), channel_id=1, source_target_pairs={{0,1},{1,0},{2,3},{3,2},{4,5},{5,4},{6,7},{7,6},{8,9},{9,8},{10,11... | collective-permute-start | bytes 1966088 | tf_op jit(solution)/shard_map/ppermute | solution.py:20
  82.9 40.7 %collective-permute-start.22 = (bf16[1280,640]{1,0:T(8,128)(2,1)S(1)}, bf16[1280,640]{1,0:T(8,128)(2,1)S(1)}, u32[]{:S(2)}, u32[]{:S(2)}) collective-permute-start(bf16[1280,640]{1,0:T(8,128)(2,1)S(1)} %bitcast.40), channel_id=1, source_target_pairs={{0,1},{1,0},{2,3},{3,2},{4,5},{5,4},{6,7},{7,6},{8,9},{9,8},{10,11... | collective-permute-start | bytes 4915208 | tf_op jit(solution)/shard_map/ppermute | solution.py:20
  83.1 40.6 %collective-permute-start.23 = (bf16[1280,640]{1,0:T(8,128)(2,1)S(1)}, bf16[1280,640]{1,0:T(8,128)(2,1)S(1)}, u32[]{:S(2)}, u32[]{:S(2)}) collective-permute-start(bf16[1280,640]{1,0:T(8,128)(2,1)S(1)} %bitcast.44), channel_id=1, source_target_pairs={{0,1},{1,0},{2,3},{3,2},{4,5},{5,4},{6,7},{7,6},{8,9},{9,8},{10,11... | collective-permute-start | bytes 4915208 | tf_op jit(solution)/shard_map/ppermute | solution.py:20
  91.4 2.2 %collective-permute-start.7 = (bf16[512,256]{1,0:T(8,128)(2,1)S(1)}, bf16[512,256]{1,0:T(8,128)(2,1)S(1)}, u32[]{:S(2)}, u32[]{:S(2)}) collective-permute-start(bf16[512,256]{1,0:T(8,128)(2,1)S(1)} %get-tuple-element.22), channel_id=1, source_target_pairs={{0,1},{1,0},{2,3},{3,2},{4,5},{5,4},{6,7},{7,6},{8,9},{9,8},{10,11... | collective-permute-start | bytes 786440 | tf_op jit(solution)/shard_map/ppermute | solution.py:20
  94.6 10.5 %collective-permute-start.10 = (bf16[128,1280]{1,0:T(8,128)(2,1)S(1)}, bf16[128,1280]{1,0:T(8,128)(2,1)S(1)}, u32[]{:S(2)}, u32[]{:S(2)}) collective-permute-start(bf16[128,1280]{1,0:T(8,128)(2,1)S(1)} %get-tuple-element.25), channel_id=1, source_target_pairs={{0,4},{2,6},{4,0},{6,2},{1,5},{3,7},{5,1},{7,3},{8,12},{10,14},{12... | collective-permute-start | bytes 983048 | tf_op jit(solution)/shard_map/ppermute | solution.py:20
  96.6 13.1 %collective-permute-start.11 = (bf16[128,1280]{1,0:T(8,128)(2,1)S(1)}, bf16[128,1280]{1,0:T(8,128)(2,1)S(1)}, u32[]{:S(2)}, u32[]{:S(2)}) collective-permute-start(bf16[128,1280]{1,0:T(8,128)(2,1)S(1)} %get-tuple-element.26), channel_id=1, source_target_pairs={{0,6},{2,0},{4,2},{6,4},{1,7},{3,1},{5,3},{7,5},{8,14},{10,8},{12,... | collective-permute-start | bytes 983048 | tf_op jit(solution)/shard_map/ppermute | solution.py:20
  97.2 15.6 %collective-permute-start.9 = (bf16[128,1280]{1,0:T(8,128)(2,1)S(1)}, bf16[128,1280]{1,0:T(8,128)(2,1)S(1)}, u32[]{:S(2)}, u32[]{:S(2)}) collective-permute-start(bf16[128,1280]{1,0:T(8,128)(2,1)S(1)} %get-tuple-element.24), channel_id=1, source_target_pairs={{0,2},{2,4},{4,6},{6,0},{1,3},{3,5},{5,7},{7,1},{8,10},{10,12},{12... | collective-permute-start | bytes 983048 | tf_op jit(solution)/shard_map/ppermute | solution.py:20
  113.2 8.9 %collective-permute-start.25 = (bf16[128,1280]{1,0:T(8,128)(2,1)S(1)}, bf16[128,1280]{1,0:T(8,128)(2,1)S(1)}, u32[]{:S(2)}, u32[]{:S(2)}) collective-permute-start(bf16[128,1280]{1,0:T(8,128)(2,1)S(1)} %get-tuple-element.28.refs_0_), channel_id=1, source_target_pairs={{0,6},{2,0},{4,2},{6,4},{1,7},{3,1},{5,3},{7,5},{8,14},{10,8},{12,... | collective-permute-start | bytes 983048 | tf_op jit(solution)/shard_map/ppermute | solution.py:20
  113.3 9.8 %collective-permute-start.26 = (bf16[128,1280]{1,0:T(8,128)(2,1)S(1)}, bf16[128,1280]{1,0:T(8,128)(2,1)S(1)}, u32[]{:S(2)}, u32[]{:S(2)}) collective-permute-start(bf16[128,1280]{1,0:T(8,128)(2,1)S(1)} %get-tuple-element.28.refs_0_), channel_id=1, source_target_pairs={{0,2},{2,4},{4,6},{6,0},{1,3},{3,5},{5,7},{7,1},{8,10},{10,12},{12... | collective-permute-start | bytes 983048 | tf_op jit(solution)/shard_map/ppermute | solution.py:20
  122.0 7.0 %collective-permute-start.29 = (bf16[64,1280]{1,0:T(8,128)(2,1)S(1)}, bf16[64,1280]{1,0:T(8,128)(2,1)S(1)}, u32[]{:S(2)}, u32[]{:S(2)}) collective-permute-start(bf16[64,1280]{1,0:T(8,128)(2,1)S(1)} %slice.45), channel_id=1, source_target_pairs={{0,6},{2,0},{4,2},{6,4},{1,7},{3,1},{5,3},{7,5},{8,14},{10,8},{12,... | collective-permute-start | bytes 491528 | tf_op jit(solution)/shard_map/ppermute | solution.py:20
  123.1 6.0 %collective-permute-start.30 = (bf16[64,1280]{1,0:T(8,128)(2,1)S(1)}, bf16[64,1280]{1,0:T(8,128)(2,1)S(1)}, u32[]{:S(2)}, u32[]{:S(2)}) collective-permute-start(bf16[64,1280]{1,0:T(8,128)(2,1)S(1)} %slice.46), channel_id=1, source_target_pairs={{0,2},{2,4},{4,6},{6,0},{1,3},{3,5},{5,7},{7,1},{8,10},{10,12},{12... | collective-permute-start | bytes 491528 | tf_op jit(solution)/shard_map/ppermute | solution.py:20
  126.3 11.8 %collective-permute-start.27 = (bf16[128,1280]{1,0:T(8,128)(2,1)S(1)}, bf16[128,1280]{1,0:T(8,128)(2,1)S(1)}, u32[]{:S(2)}, u32[]{:S(2)}) collective-permute-start(bf16[128,1280]{1,0:T(8,128)(2,1)S(1)} %get-tuple-element.31), channel_id=1, source_target_pairs={{0,2},{2,4},{4,6},{6,0},{1,3},{3,5},{5,7},{7,1},{8,10},{10,12},{12... | collective-permute-start | bytes 983048 | tf_op jit(solution)/shard_map/ppermute | solution.py:20
  126.6 11.6 %collective-permute-start.28 = (bf16[128,1280]{1,0:T(8,128)(2,1)S(1)}, bf16[128,1280]{1,0:T(8,128)(2,1)S(1)}, u32[]{:S(2)}, u32[]{:S(2)}) collective-permute-start(bf16[128,1280]{1,0:T(8,128)(2,1)S(1)} %get-tuple-element.32), channel_id=1, source_target_pairs={{0,6},{2,0},{4,2},{6,4},{1,7},{3,1},{5,3},{7,5},{8,14},{10,8},{12,... | collective-permute-start | bytes 983048 | tf_op jit(solution)/shard_map/ppermute | solution.py:20
  131.0 11.4 %collective-permute-start.31 = (bf16[128,1280]{1,0:T(8,128)(2,1)S(1)}, bf16[128,1280]{1,0:T(8,128)(2,1)S(1)}, u32[]{:S(2)}, u32[]{:S(2)}) collective-permute-start(bf16[128,1280]{1,0:T(8,128)(2,1)S(1)} %shard_map.120), channel_id=1, source_target_pairs={{0,4},{2,6},{4,0},{6,2},{1,5},{3,7},{5,1},{7,3},{8,12},{10,14},{12... | collective-permute-start | bytes 983048 | tf_op jit(solution)/shard_map/ppermute | solution.py:20
  (14 other events, 105.0 us)
